TPU v7x, 32 devices: a whole 2x2x4 slice. The times are simulated.
32 devices in a mesh: cells: 8 (over z, y), grp: 4 (over x, core).
Axes of the slice: x: 2, y: 2, z: 4, core: 2. Of those that a mesh axis runs over, the one named last changes fastest.
Arguments:
- latent_coordinates: float32 [50, 131072], P(None, ('cells', 'grp')), may hold values from -40 to 40
- group_means: float32 [16, 50], replicated, may hold values from -4 to 4
- entropy_scaling: float32 [16], replicated, may hold values from 0.5 to 2
- sample_shrinkage_lambda: float32 [200], replicated, may hold values from 164 to 1310
- sample_population: int32 [200], replicated, may hold values from 1 to 1310, 131072 in all
Outputs:
- corrected: float32 [50, 131072], P(None, ('cells', 'grp'))
- new_centroids: float32 [16, 50], P('cells')
All inputs are finite; a program needn't handle non-finite values.
Results may differ from a plain program's by a relative error of at most 0.0003.
Values sent between devices are 32-bit elements; how exact they have to be, the bound alone decides.
No kernel may reach another device: no remote copies, remote signals or barrier semaphores. Data moves between devices by JAX's collectives and lax.ppermute only.
A program may use at most 64 MiB of HBM per device.

v0:
```python
import jax
import jax.numpy as jnp
from jax import lax
from jax.sharding import PartitionSpec as P

diversity = 2.0
intercept_ridge = 1.0
highest = lax.Precision.HIGHEST


def from_behind(block, axis, distance):
    devices = range(lax.axis_size(axis))
    route = [(i - distance, i) for i in devices if i - distance in devices]
    return lax.ppermute(block, axis, route)


def observation_affinity(latent_coordinates, group_means, entropy_scaling):
    pairwise_dots = jnp.dot(
        group_means, latent_coordinates, precision=highest, preferred_element_type=jnp.float32
    )
    quadratic_lengths = jnp.sum(group_means * group_means, axis=1)
    return (2.0 * pairwise_dots - quadratic_lengths[:, None]) / (2.0 * entropy_scaling[:, None])


def probabilistic_responsibility(group_affinity):
    top = jnp.max(group_affinity, axis=0, keepdims=True)
    raised = jnp.exp(group_affinity - top)
    return raised / jnp.sum(raised, axis=0, keepdims=True)


def batch_parts(moments, ridge):
    mass = moments[:, 0, :]
    sums = moments[:, 1:, :]
    shrink = ridge[None, :] / (mass + ridge[None, :])
    weight = jnp.sum(mass * shrink, axis=1)
    right_side = jnp.sum(sums * shrink[:, None, :], axis=2)
    return (weight, right_side, jnp.sum(mass, axis=1), jnp.sum(sums, axis=2))


def slopes_of(moments, ridge, weight, right_side):
    mass = moments[:, 0, :]
    sums = moments[:, 1:, :]
    intercept = right_side / (intercept_ridge + weight)[:, None]
    return (sums - mass[:, None, :] * intercept[:, :, None]) / (mass + ridge[None, :])[:, None, :]


def body(
    latent_coordinates, group_means, entropy_scaling, sample_shrinkage_lambda, sample_population
):
    local_cells = latent_coordinates.shape[1]
    num_pcs = latent_coordinates.shape[0]
    clusters = group_means.shape[0]
    batches = sample_population.shape[0]
    owned = clusters // lax.axis_size("cells")
    offset = (lax.axis_index("cells") * lax.axis_size("grp") + lax.axis_index("grp")) * local_cells
    batch_ends = jnp.cumsum(sample_population)
    batch_starts = batch_ends - sample_population
    cells_total = jnp.sum(sample_population).astype(jnp.float32)
    position = offset + lax.iota(jnp.int32, local_cells)
    batch_of = jnp.sum((batch_ends[:, None] <= position[None, :]).astype(jnp.int32), axis=0)
    first_batch = batch_of[0]
    last_batch = batch_of[local_cells - 1]
    group_affinity = observation_affinity(latent_coordinates, group_means, entropy_scaling)
    expected_occupancy = probabilistic_responsibility(group_affinity)

    def count_step(batch_id, running):
        in_batch = (batch_of == batch_id).astype(jnp.float32)
        single_observation = jnp.dot(
            expected_occupancy, in_batch, precision=highest, preferred_element_type=jnp.float32
        )
        return lax.dynamic_update_slice(
            running, single_observation[:, None], (jnp.int32(0), batch_id)
        )

    counts = lax.fori_loop(
        first_batch, last_batch + 1, count_step, jnp.zeros((clusters, batches), jnp.float32)
    )
    counts = lax.psum(counts, ("cells", "grp"))
    totals = jnp.sum(counts, axis=1)
    expected = sample_population.astype(jnp.float32)[None, :] * totals[:, None] / cells_total
    penalty = diversity * jnp.log((counts + 1.0) / (expected + 1.0))

    def penalty_step(batch_id, running):
        in_batch = (batch_of == batch_id).astype(jnp.float32)
        column = lax.dynamic_index_in_dim(penalty, batch_id, 1, keepdims=True)
        return running + column * in_batch[None, :]

    cell_penalty = lax.fori_loop(
        first_batch, last_batch + 1, penalty_step, jnp.zeros((clusters, local_cells), jnp.float32)
    )
    assign = probabilistic_responsibility(group_affinity - cell_penalty)
    augmented = jnp.concatenate(
        [jnp.ones((1, local_cells), jnp.float32), latent_coordinates], axis=0
    )

    def moment_step(batch_id, running):
        in_batch = (batch_of == batch_id).astype(jnp.float32)
        contiguous_portion = jnp.einsum(
            "kn,dn->kd", assign * in_batch[None, :], augmented, precision=highest
        )
        return lax.dynamic_update_slice(
            running, contiguous_portion[:, :, None], (jnp.int32(0), jnp.int32(0), batch_id)
        )

    moments = lax.fori_loop(
        first_batch,
        last_batch + 1,
        moment_step,
        jnp.zeros((clusters, num_pcs + 1, batches), jnp.float32),
    )
    devices_flat = lax.axis_size("cells") * lax.axis_size("grp")
    most_cells = 2 * local_cells * devices_flat // batches
    reach = (most_cells - 2) // local_cells + 1
    begins_here = (batch_starts >= offset) & (batch_starts < offset + local_cells)
    owner_mask = begins_here.astype(jnp.float32)
    head_owned = begins_here[first_batch]
    head_column = lax.dynamic_index_in_dim(moments, first_batch, 2, keepdims=False)
    sent_stats = jnp.where(head_owned, 0.0, 1.0) * head_column
    sent_tag = jnp.where(head_owned, 0.0, first_batch.astype(jnp.float32) + 1.0) * jnp.ones(
        (1,), jnp.float32
    )
    completed = moments
    for hop in range(1, reach + 1):
        got_stats, got_tag = from_behind((sent_stats, sent_tag), ("cells", "grp"), -hop)
        got_id = jnp.maximum(got_tag[0].astype(jnp.int32) - 1, 0)
        accept = jnp.where((got_tag[0] > 0.5) & begins_here[got_id], 1.0, 0.0)
        single_observation = (
            lax.dynamic_index_in_dim(completed, got_id, 2, keepdims=False) + accept * got_stats
        )
        completed = lax.dynamic_update_slice(
            completed, single_observation[:, :, None], (jnp.int32(0), jnp.int32(0), got_id)
        )
    completed = completed * owner_mask[None, None, :]
    weight, right_side, mass_total, moment_total = lax.psum(
        batch_parts(completed, sample_shrinkage_lambda), ("cells", "grp")
    )
    coefficients = slopes_of(completed, sample_shrinkage_lambda, weight, right_side)
    every_centroid = moment_total / (1.0 + mass_total)[:, None]
    new_centroids = lax.dynamic_slice_in_dim(
        every_centroid, lax.axis_index("cells") * owned, owned, 0
    )
    tail_owned = begins_here[last_batch]
    tail_column = lax.dynamic_index_in_dim(coefficients, last_batch, 2, keepdims=False)
    tail_send = jnp.where(tail_owned, 1.0, 0.0) * tail_column
    tail_tag = jnp.where(tail_owned, last_batch.astype(jnp.float32) + 1.0, 0.0) * jnp.ones(
        (1,), jnp.float32
    )
    head_fix = jnp.zeros_like(tail_column)
    for hop in range(1, reach + 1):
        got_coef, got_tag = from_behind((tail_send, tail_tag), ("cells", "grp"), hop)
        match = got_tag[0] == first_batch.astype(jnp.float32) + 1.0
        head_fix = jnp.where(match, got_coef, head_fix)
    own_head = lax.dynamic_index_in_dim(coefficients, first_batch, 2, keepdims=False)
    head_final = jnp.where(head_owned, own_head, head_fix)
    coefficients = lax.dynamic_update_slice(
        coefficients, head_final[:, :, None], (jnp.int32(0), jnp.int32(0), first_batch)
    )

    def correct_step(batch_id, running):
        in_batch = (batch_of == batch_id).astype(jnp.float32)
        slope_table = lax.dynamic_index_in_dim(coefficients, batch_id, 2, keepdims=False)
        moved = jnp.einsum("kd,kn->dn", slope_table, assign * in_batch[None, :], precision=highest)
        return running - moved

    corrected = lax.fori_loop(first_batch, last_batch + 1, correct_step, latent_coordinates)
    return (corrected, new_centroids)


def solution(mesh):
    return jax.shard_map(
        body,
        mesh=mesh,
        in_specs=(P(None, ("cells", "grp")), P(), P(), P(), P()),
        out_specs=(P(None, ("cells", "grp")), P("cells", None)),
        check_vma=False,
    )
```

profile of v0, /device:TPU:28, one launch (start us, length us, event | category | flops | bytes accessed | tf_op | source)
XLA Modules:
  0.0 234.1 jit_solution(691053589172839008)
XLA Ops:
  0.7 1.2 copy.75
  6.1 0.6 dynamic_slice.34
  7.4 4.1 %collective-permute-start = (f32[1]{0:T(128)}, f32[1]{0:T(128)}, u32[]{:S(2)}, u32[]{:S(2)}) collective-permute-start(f32[1]{0:T(128)} %bitcast.10), channel_id=1, source_target_pairs={{1,0},{2,1},{3,2},{4,3},{5,4},{6,5},{7,6},{8,7},{9,8},{10,9},{11,1... | collective-permute-start | bytes 20 | tf_op jit(solution)/shard_map/ppermute | solution.py:14
  12.1 0.6 fusion.19
  16.3 4.0 %while.40 = (s32[]{:T(128)}, f32[16,200]{0,1:T(8,128)S(1)}, s32[]{:T(128)}, s32[4096]{0:T(1024)S(1)}, f32[16,4096]{1,0:T(8,128)S(1)}, /*index=5*/s32[]{:T(128)}, s32[]{:T(128)}, s32[]{:T(128)}) while((s32[]{:T(128)}, f32[16,200]{0,1:T(8,128)S(1)}, s32[]{:T(128)}, s32[4096]{0:T(1024)S(1)}, f32[16,4096]{1,0:T(8,128)S(1)}, /*index=5*/s32[]{:T(128)}, ...), condition=%wide.region_7.8_spmd, body=%wide.region_6.7_spmd.sunk | while | flops 790533 | bytes 295231 | solution.py:75
  20.3 39.9 %psum.35 = f32[16,200]{0,1:T(8,128)S(1)} all-reduce(f32[16,200]{0,1:T(8,128)S(1)} %get-tuple-element.124), channel_id=1, replica_groups=mesh['cells'=8,'grp'=4] {'cells','grp'}, use_global_device_ids=true, to_apply=%region_8.9 | all-reduce | flops 3200 | bytes 25600 | tf_op jit(solution)/shard_map/psum | solution.py:78
  61.0 1.8 while.41
  63.0 1.3 broadcast_in_dim.18
  64.3 15.7 %while.42 = (s32[]{:T(128)}, f32[16,51,200]{1,0,2:T(8,128)}, s32[]{:T(128)}, s32[4096]{0:T(1024)S(1)}, f32[16,4096]{1,0:T(8,128)S(1)}, /*index=5*/f32[51,4096]{1,0:T(8,128)S(1)}, s32[]{:T(128)}, s32[]{:T(128)}, s32[]{:T(128)}) while((s32[]{:T(128)}, f32[16,51,200]{1,0,2:T(8,128)}, s32[]{:T(128)}, s32[4096]{0:T(1024)S(1)}, ...), condition=%wide.region_16.17_spmd, body=%wide.region_15.16_spmd.sunk | while | flops 40181764 | bytes 1155207 | solution.py:105
  64.3 1.4 fusion.38
  65.7 1.4 fusion.38
  67.1 1.4 fusion.38
  68.6 1.4 fusion.38
  70.0 1.4 fusion.38
  71.4 1.4 fusion.38
  72.9 1.4 fusion.38
  74.3 1.4 fusion.38
  75.7 1.4 fusion.38
  77.1 1.4 fusion.38
  78.6 1.4 fusion.38
  80.6 0.7 multiply_bitcast_fusion.1
  81.3 1.9 collective-permute-start.1
  85.8 0.6 fusion.20
  87.7 3.3 %collective-permute-start.2 = (f32[1]{0:T(128)}, f32[1]{0:T(128)}, u32[]{:S(2)}, u32[]{:S(2)}) collective-permute-start(f32[1]{0:T(128)} %bitcast.24), channel_id=1, source_target_pairs={{0,1},{1,2},{2,3},{3,4},{4,5},{5,6},{6,7},{7,8},{8,9},{9,10},{10,1... | collective-permute-start | bytes 20 | tf_op jit(solution)/shard_map/ppermute | solution.py:14
  92.2 1.4 collective-permute-done.2
  94.2 0.6 bitcast_dynamic-update-slice_fusion.1
  94.9 1.7 broadcast_multiply_fusion
  96.6 2.8 %slice_reduce_fusion.2 = (f32[16]{0:T(128)S(1)}, f32[16,1,200]{1,0,2:T(8,128)}, f32[16,1,200]{1,0,2:T(8,128)}, f32[16,1,200]{1,0,2:T(8,128)}) fusion(f32[16,51,200]{1,0,2:T(8,128)S(1)} %broadcast_multiply_fusion, f32[200]{0:T(256)S(1)} %copy-done.5), kind=kLoop, calls=%fused_computation.57 | loop fusion | flops 9584 | bytes 52064 | tf_op jit(solution)/shard_map/reduce_sum | solution.py:37
  99.4 2.2 copy.34
  101.6 2.6 %copy.42 = f32[16,1,200]{0,2,1:T(8,128)S(1)} copy(f32[16,1,200]{1,0,2:T(8,128)} %get-tuple-element.217) | data formatting | bytes 25600 | tf_op jit(solution)/shard_map/mul | solution.py:44
  104.2 2.7 %copy.43 = f32[16,1,200]{0,2,1:T(8,128)S(1)} copy(f32[16,1,200]{1,0,2:T(8,128)} %get-tuple-element.219) | data formatting | bytes 25600 | tf_op jit(solution)/shard_map/mul | solution.py:36
  106.9 2.4 %slice_reduce_fusion = (f32[16,50]{1,0:T(8,128)S(1)}, f32[16,50]{1,0:T(8,128)S(1)}) fusion(f32[16,51,200]{1,0,2:T(8,128)} %copy-done.1, f32[16,200]{0,1:T(8,128)S(1)} %bitcast.75), kind=kLoop, calls=%fused_computation.23 | loop fusion | flops 478400 | bytes 659200 | tf_op jit(solution)/shard_map/reduce_sum | solution.py:37
  109.5 2.7 %copy.44 = f32[16,1,200]{0,2,1:T(8,128)S(1)} copy(f32[16,1,200]{1,0,2:T(8,128)} %get-tuple-element.218) | data formatting | bytes 25600 | tf_op jit(solution)/shard_map/div | solution.py:44
  112.1 41.6 %all-reduce.2 = (f32[16,50]{1,0:T(8,128)S(1)}, f32[16]{0:T(128)S(1)}, f32[16,50]{0,1:T(8,128)S(1)}, f32[16]{0:T(128)S(1)}) all-reduce(f32[16,50]{1,0:T(8,128)S(1)} %get-tuple-element.159, f32[16]{0:T(128)S(1)} %fusion.14, f32[16,50]{0,1:T(8,128)S(1)} %copy.45, ...), channel_id=1, replica_groups=mesh['cells'=8,'grp'=4] {'cells','grp'}, use_global_device_ids=true, to_apply=%region_18.19 | all-reduce | flops 1632 | bytes 13056 | tf_op jit(solution)/shard_map/psum | solution.py:134
  153.8 2.6 %subtract_divide_fusion = f32[16,50,200]{1,0,2:T(8,128)S(1)} fusion(f32[16,51,200]{1,0,2:T(8,128)} %copy-done.1, f32[16,200]{0,1:T(8,128)S(1)} %bitcast.77, f32[16,50]{1,0:T(8,128)S(1)} %broadcast_divide_fusion.1, f32[16,200]{0,1:T(8,128)S(1)} %bitcast.76), kind=kLoop, calls=%fused_computation.21 | loop fusion | flops 480000 | bytes 1308800 | tf_op jit(solution)/shard_map/div | solution.py:44
  156.5 1.2 copy-done.2
  157.6 1.9 collective-permute-start.3
  159.7 0.6 copy.41
  160.4 3.1 %collective-permute-done.3 = f32[16,50]{1,0:T(8,128)S(1)} collective-permute-done((f32[16,50]{1,0:T(8,128)S(1)}, f32[16,50]{1,0:T(8,128)S(1)}, u32[]{:S(2)}, u32[]{:S(2)}) %collective-permute-start.3) | collective-permute-done | bytes 3232 | tf_op jit(solution)/shard_map/ppermute | solution.py:14
  163.5 1.2 bitcast_dynamic-update-slice_fusion
  164.7 68.5 %while.43 = (s32[]{:T(128)}, f32[50,4096]{1,0:T(8,128)S(1)}, s32[]{:T(128)}, f32[16,50,200]{1,0,2:T(8,128)}, s32[4096]{0:T(1024)S(1)}, /*index=5*/f32[16,4096]{1,0:T(8,128)S(1)}, s32[]{:T(128)}, s32[]{:T(128)}, s32[]{:T(128)}) while((s32[]{:T(128)}, f32[50,4096]{1,0:T(8,128)S(1)}, s32[]{:T(128)}, f32[16,50,200]{1,0,2:T(8,128)}, ...), condition=%wide.region_22.23_spmd, body=%wide.region_21.22_spmd.sunk | while | flops 39600132 | bytes 1958023 | solution.py:165
  167.3 0.6 compare_convert_fusion.8
  168.0 1.8 convolution_subtract_fusion.2
  173.5 0.6 compare_convert_fusion.8
  174.1 1.8 convolution_subtract_fusion.2
  179.7 0.6 compare_convert_fusion.8
  180.3 1.8 convolution_subtract_fusion.2
  185.8 0.6 compare_convert_fusion.8
  186.5 1.8 convolution_subtract_fusion.2
  192.0 0.6 compare_convert_fusion.8
  192.6 1.8 convolution_subtract_fusion.2
  198.1 0.6 compare_convert_fusion.8
  198.8 1.8 convolution_subtract_fusion.2
  204.3 0.6 compare_convert_fusion.8
  205.0 1.8 convolution_subtract_fusion.2
  210.5 0.6 compare_convert_fusion.8
  211.1 1.8 convolution_subtract_fusion.2
  216.6 0.6 compare_convert_fusion.8
  217.3 1.8 convolution_subtract_fusion.2
  222.8 0.6 compare_convert_fusion.8
  223.5 1.8 convolution_subtract_fusion.2
  229.0 0.6 compare_convert_fusion.8
  229.6 1.8 convolution_subtract_fusion.2
  233.2 0.9 copy-done
  (132 shorter events, 8.2 us)
Async XLA Ops:
  0.6 14.0 %copy-start.3 = (f32[16,50]{1,0:T(8,128)S(1)}, f32[16,50]{1,0:T(8,128)}, u32[]{:S(2)}) copy-start(f32[16,50]{1,0:T(8,128)} %param.14) | copy-start | bytes 9604
  0.6 14.0 %copy-start.6 = (f32[16]{0:T(128)S(1)}, f32[16]{0:T(128)}, u32[]{:S(2)}) copy-start(f32[16]{0:T(128)} %param.15) | copy-start | bytes 196
  0.7 1.2 copy-start.4
  7.4 72.6 %collective-permute-start = (f32[1]{0:T(128)}, f32[1]{0:T(128)}, u32[]{:S(2)}, u32[]{:S(2)}) collective-permute-start(f32[1]{0:T(128)} %bitcast.10), channel_id=1, source_target_pairs={{1,0},{2,1},{3,2},{4,3},{5,4},{6,5},{7,6},{8,7},{9,8},{10,9},{11,1... | collective-permute-start | bytes 20 | tf_op jit(solution)/shard_map/ppermute | solution.py:14
  81.3 13.0 %collective-permute-start.1 = (f32[16,51]{1,0:T(8,128)S(1)}, f32[16,51]{1,0:T(8,128)S(1)}, u32[]{:S(2)}, u32[]{:S(2)}) collective-permute-start(f32[16,51]{1,0:T(8,128)S(1)} %get-tuple-element.220), channel_id=1, source_target_pairs={{1,0},{2,1},{3,2},{4,3},{5,4},{6,5},{7,6},{8,7},{9,8},{10,9},{11,1... | collective-permute-start | bytes 9800 | tf_op jit(solution)/shard_map/ppermute | solution.py:14
  87.7 5.9 %collective-permute-start.2 = (f32[1]{0:T(128)}, f32[1]{0:T(128)}, u32[]{:S(2)}, u32[]{:S(2)}) collective-permute-start(f32[1]{0:T(128)} %bitcast.24), channel_id=1, source_target_pairs={{0,1},{1,2},{2,3},{3,4},{4,5},{5,6},{6,7},{7,8},{8,9},{9,10},{10,1... | collective-permute-start | bytes 20 | tf_op jit(solution)/shard_map/ppermute | solution.py:14
  94.8 1.7 copy-start.5
  96.6 2.8 %copy-start.1 = (f32[16,51,200]{1,0,2:T(8,128)}, f32[16,51,200]{1,0,2:T(8,128)S(1)}, u32[]{:S(2)}) copy-start(f32[16,51,200]{1,0,2:T(8,128)S(1)} %broadcast_multiply_fusion) | copy-start | bytes 1958404
  156.4 1.2 copy-start.2
  157.6 5.9 %collective-permute-start.3 = (f32[16,50]{1,0:T(8,128)S(1)}, f32[16,50]{1,0:T(8,128)S(1)}, u32[]{:S(2)}, u32[]{:S(2)}) collective-permute-start(f32[16,50]{1,0:T(8,128)S(1)} %get-tuple-element.214), channel_id=1, source_target_pairs={{0,1},{1,2},{2,3},{3,4},{4,5},{5,6},{6,7},{7,8},{8,9},{9,10},{10,1... | collective-permute-start | bytes 9608 | tf_op jit(solution)/shard_map/ppermute | solution.py:14
  233.2 0.9 copy-start
where the time goes:
time: 230 us; the launch traced here: 234 us
  blocking collectives  81.5 us (35%)
  loops' own time  43.1 us (19%)
  matrix products  38.2 us (17%)
  other arithmetic  22.9 us (10%)
  local copies, waits for them, and re-layouts  18.5 us (8%)
  between operations  14.2 us (6%)
  starting transfers between devices  11.2 us (5%)
  waiting for transfers between devices  4.52 us (2%)
    another operation x1, loops' own time, body(): lax.fori_loop(first_batch, last_batch + 1, correct_step, latent_coordinates)  42.1 us
    psum x1, blocking collectives, body(): lax.psum(batch_parts(completed, sample_shrinkage_lambda), ('cells', 'grp'))  41.6 us
    psum x1, blocking collectives, body(): counts = lax.psum(counts, ('cells', 'grp'))  39.9 us
    dot_general x11, matrix products, correct_step(): jnp.einsum('kd,kn->dn', slope_table, assign * in_batch[None, :], precisio...  19.3 us
    dot_general x11, matrix products, moment_step(): jnp.einsum('kn,dn->kd', assign * in_batch[None, :], augmented, precision=...  15.7 us
    ppermute x4, starting transfers between devices, from_behind(): return lax.ppermute(block, axis, route)  11.2 us
    convert_element_type x11, other arithmetic, correct_step(): in_batch = (batch_of == batch_id).astype(jnp.float32)  7.13 us
    reduce_sum x2, other arithmetic, batch_parts(): return (weight, right_side, jnp.sum(mass, axis=1), jnp.sum(sums, axis=2))  5.2 us
  transfers between devices with their start and end apart: 4, of which 2 were waited for; matrix products, arithmetic and copies ran while one was open for 11% of the time, Pallas kernels for 0%

commit v1 on v0

v1 whole, which is shorter than its diff:
```python
import jax
import jax.numpy as jnp
from jax import lax
from jax.experimental import pallas as pl
from jax.experimental.pallas import tpu as pltpu
from jax.sharding import PartitionSpec as P

f32 = jnp.float32
bf16 = jnp.bfloat16
HALF = 64
LANES = 128
AXES = ("cells", "grp")


def split(value):
    high = value.astype(bf16)
    return high, (value - high.astype(f32)).astype(bf16)


def iota(shape, axis):
    return lax.broadcasted_iota(jnp.int32, shape, axis)


def lane_of(value, lane):
    return jnp.broadcast_to(value[:, lane : lane + 1], value.shape)


def halves(value, lane):
    left = iota(value.shape, 1) < HALF
    return jnp.where(left, lane_of(value, lane), lane_of(value, HALF + lane))


def column(row, first, count):
    shape = (count, row.shape[1])
    pick = iota(shape, 1) == iota(shape, 0) + first
    return jnp.sum(jnp.where(pick, jnp.broadcast_to(row, shape), 0.0), axis=1, keepdims=True)


def pack_pairs(ref):
    pairs = ref.shape[0] // 2
    even = ref[pl.ds(0, pairs, stride=2), :]
    odd = ref[pl.ds(1, pairs, stride=2), :]
    return jnp.where(iota(even.shape, 1) < HALF, even, odd)


def unpack_pairs(ref, tile):
    pairs = tile.shape[0]
    left = iota(tile.shape, 1) < HALF
    turned = pltpu.roll(tile, HALF, 1)
    ref[pl.ds(0, pairs, stride=2), :] = jnp.where(left, tile, turned)
    ref[pl.ds(1, pairs, stride=2), :] = jnp.where(left, turned, tile)
    return ref[...]


def repeat(count, step):
    if count <= 8:
        for i in range(count):
            step(i, 0)
    else:
        lax.fori_loop(0, count, step, 0)


class Plan:
    def __init__(self, x, means, pop):
        self.dims, self.cells = x.shape
        self.clusters = means.shape[0]
        self.batches = pop.shape[0]
        self.rows = lax.axis_size("cells")
        self.cols = lax.axis_size("grp")
        self.devices = self.rows * self.cols
        self.total = self.cells * self.devices
        self.most = 2 * self.total // self.batches
        self.reach = (self.most - 2) // self.cells + 1
        outside = -(-(self.total - self.cells) // self.most)
        local = min(self.batches, self.batches - outside + 2)
        self.group = max(1, LANES // self.clusters)
        self.groups = -(-local // self.group)
        self.depth = self.group * self.clusters
        self.blocks = -(-(self.groups * self.group) // LANES)
        self.first_at = self.batches + self.group
        self.table = self.first_at + 2
        self.width = -(-(3 * self.clusters + 4) // LANES) * LANES
        self.pairs = self.clusters // 2
        self.gap = HALF - (self.dims + 1)
        self.gap_rows = -(-(self.dims + 1) // self.gap)
        self.owned_pairs = self.clusters // self.rows // 2

    def offset(self):
        place = lax.axis_index("cells") * self.cols + lax.axis_index("grp")
        return place * self.cells


def segment(plan, starts, offset, index):
    batch = starts[plan.first_at] + index
    return starts[batch] - offset, starts[batch + 1] - offset


def padded(plan, x_ref, xs_ref):
    low = plan.dims // 8 * 8
    tail = (xs_ref.shape[0] - low, plan.cells)
    xs_ref[low:, :] = jnp.where(iota(tail, 0) == plan.dims - low, 1.0, 0.0)
    xs_ref[0 : plan.dims, :] = x_ref[...]


def count_kernel(plan, pop, lam, scale, means, x_ref, send, prior, counts, starts, xs, ms):
    k = plan.clusters
    offset = plan.offset()
    running, first, last = jnp.int32(0), jnp.int32(0), jnp.int32(0)
    for b in range(plan.batches):
        starts[b] = running
        running = running + pop[b]
        first = first + (running <= offset).astype(jnp.int32)
        last = last + (running <= offset + plan.cells - 1).astype(jnp.int32)
    for b in range(plan.batches, plan.first_at):
        starts[b] = running
    starts[plan.first_at] = first
    starts[plan.first_at + 1] = last
    segments = last - first + 1

    padded(plan, x_ref, xs)
    ms[...] = jnp.zeros_like(ms)
    ms[:, 0 : plan.dims] = means[...]
    m = ms[...]
    m1 = m.astype(bf16).astype(f32)
    m2 = (m - m1).astype(bf16).astype(f32)
    m3 = m - m1 - m2
    zero = jnp.zeros_like(m)

    def twice(value):
        return value + pltpu.roll(value, HALF, 1)

    weights = jnp.concatenate(
        [
            jnp.concatenate([twice(m1), m1], axis=1),
            jnp.concatenate([twice(m2), zero], axis=1),
            jnp.concatenate([m3, zero], axis=1),
        ],
        axis=0,
    ).astype(bf16)
    lengths = jnp.sum(m * m, axis=1, keepdims=True)
    soft = jnp.zeros((k, 1), f32)
    row = iota((k, 1), 0)
    for c in range(k):
        soft = jnp.where(row == c, scale[c], soft)
    inverse = 1.0 / (2.0 * soft)
    chunk = min(plan.cells, 1024)
    for c in range(plan.cells // chunk):
        at = slice(c * chunk, (c + 1) * chunk)
        x = xs[:, at]
        x1 = x.astype(bf16)
        r = x - x1.astype(f32)
        x2 = r.astype(bf16)
        x3 = (r - x2.astype(f32)).astype(bf16)
        stacked = jnp.concatenate([x1, x2, x3, jnp.zeros_like(x1)], axis=0)
        dots = jnp.dot(weights, stacked, preferred_element_type=f32)
        dots = dots[0:k] + dots[k : 2 * k] + dots[2 * k : 3 * k]
        scores = (2.0 * dots - lengths) * inverse
        raised = jnp.exp(scores - jnp.max(scores, axis=0, keepdims=True))
        prior[:, at] = raised / jnp.sum(raised, axis=0, keepdims=True)

    counts[...] = jnp.zeros_like(counts)
    lane = iota((k, LANES), 1)
    cell = iota((1, plan.cells), 1)
    step = min(4, plan.group)

    def count(i, carry):
        block = lax.div(i * step, LANES)
        held = counts[block]
        for j in range(step):
            s = i * step + j
            lo, hi = segment(plan, starts, offset, jnp.minimum(s, segments - 1))
            inside = (cell >= lo) & (cell < hi)
            mine = jnp.sum(jnp.where(inside, prior[...], 0.0), axis=1, keepdims=True)
            held = jnp.where(lane == s - block * LANES, mine, held)
        counts[block] = held
        return carry

    lax.fori_loop(0, lax.div(segments + step - 1, step), count, 0)

    total = jnp.sum(prior[...], axis=1, keepdims=True)
    here = segments - 1
    tail = counts[lax.div(here, LANES)]
    last_count = jnp.sum(
        jnp.where(lane == lax.rem(here, LANES), tail, 0.0), axis=1, keepdims=True
    )
    first_count = jnp.where(segments > 1, counts[0][:, 0:1], 0.0)
    wide = (k, plan.width)
    place = iota(wide, 1) - iota(wide, 0)
    out = jnp.where(place == 0, total, 0.0)
    out = jnp.where(place == k, first_count, out)
    out = jnp.where(place == 2 * k, last_count, out)
    out = jnp.sum(out, axis=0, keepdims=True)
    lanes = iota((1, plan.width), 1)
    out = jnp.where(lanes == 3 * k, first.astype(f32), out)
    out = jnp.where(lanes == 3 * k + 1, last.astype(f32), out)
    out = jnp.where(lanes == 3 * k + 2, lam[first], out)
    out = jnp.where(lanes == 3 * k + 3, lam[last], out)
    send[...] = jnp.broadcast_to(out, send.shape)


def masked(plan, a1, a2, stack, starts, offset, group):
    k = plan.clusters
    cell = iota((k, plan.cells), 1)
    for j in range(plan.group):
        lo, hi = segment_in(plan, starts, offset, group * plan.group + j)
        inside = jnp.where((cell >= lo) & (cell < hi), 1.0, 0.0).astype(bf16)
        stack[j * k : (j + 1) * k, :] = a1[...] * inside
        stack[plan.depth + j * k : plan.depth + (j + 1) * k, :] = a2[...] * inside


def segment_in(plan, starts, offset, index):
    batch = jnp.minimum(starts[plan.first_at] + index, plan.first_at - 1)
    following = jnp.minimum(batch + 1, plan.first_at - 1)
    return starts[batch] - offset, starts[following] - offset


def moment_kernel(
    plan, starts, lam, got, prior, counts, x_ref, send, assign, moments, xs, wide, a1, a2, stack, sums, turned
):
    k = plan.clusters
    offset = plan.offset()
    first, last = starts[plan.first_at], starts[plan.first_at + 1]
    segments = last - first + 1
    groups = lax.div(segments + plan.group - 1, plan.group)
    padded(plan, x_ref, xs)

    table = got[...]
    total = column(jnp.sum(table, axis=0, keepdims=True), 0, k)
    heads, tails = table[:, 3 * k : 3 * k + 1], table[:, 3 * k + 1 : 3 * k + 2]

    def complete(batch):
        batch = batch.astype(f32)
        of_heads = jnp.sum(jnp.where(heads == batch, table, 0.0), axis=0, keepdims=True)
        of_tails = jnp.sum(jnp.where(tails == batch, table, 0.0), axis=0, keepdims=True)
        return column(of_heads, k, k) + column(of_tails, 2 * k, k)

    first_count, last_count = complete(first), complete(last)
    share = total / f32(plan.total)
    cell = iota((1, plan.cells), 1)
    lane = iota((k, LANES), 1)
    wide[...] = jnp.zeros_like(wide)

    def weigh(g, carry):
        block = lax.div(g * plan.group, LANES)
        held = counts[block]
        for j in range(plan.group):
            s = g * plan.group + j
            lo, hi = segment_in(plan, starts, offset, s)
            mine = jnp.sum(
                jnp.where(lane == s - block * LANES, held, 0.0), axis=1, keepdims=True
            )
            mine = jnp.where(s == 0, first_count, mine)
            mine = jnp.where(s == segments - 1, last_count, mine)
            expected = (hi - lo).astype(f32) * share
            ratio = (expected + 1.0) / (mine + 1.0)
            inside = (cell >= lo) & (cell < hi)
            wide[...] = jnp.where(inside, ratio * ratio, wide[...])
        return carry

    lax.fori_loop(0, groups, weigh, 0)
    raised = prior[...] * wide[...]
    chosen = raised / jnp.sum(raised, axis=0, keepdims=True)
    assign[...] = chosen
    a1[...], a2[...] = split(chosen)
    x1, x2 = split(xs[...])
    cellwise = jnp.concatenate([x1, x2], axis=0)

    sums[...] = jnp.zeros_like(sums)

    def gather(g, carry):
        masked(plan, a1, a2, stack, starts, offset, g)
        both = lax.dot_general(
            stack[...], cellwise, (((1,), (1,)), ((), ())), preferred_element_type=f32
        )
        both = both[0 : plan.depth] + both[plan.depth :]
        both = both + pltpu.roll(both, HALF, 1)
        moments[pl.ds(pl.multiple_of(g * plan.depth, plan.depth), plan.depth), :] = both
        mass = lane_of(both, plan.dims)
        inner, head, tail, every = sums[0], sums[1], sums[2], sums[3]
        for j in range(plan.group):
            s = g * plan.group + j
            at = slice(j * k, (j + 1) * k)
            ridge = lam[jnp.minimum(first + s, plan.batches - 1)]
            part = both[at]
            every = every + part
            shrunk = part * (ridge / (mass[at] + ridge))
            inner = inner + jnp.where((s > 0) & (s < segments - 1), shrunk, 0.0)
            head = head + jnp.where((s == 0) & (segments > 1), part, 0.0)
            tail = tail + jnp.where(s == segments - 1, part, 0.0)
        sums[0], sums[1], sums[2], sums[3] = inner, head, tail, every
        return carry

    lax.fori_loop(0, groups, gather, 0)
    inner, head, tail, every = [pack_pairs(sums.at[i]) for i in range(4)]
    lanes = lax.rem(iota(inner.shape, 1), HALF)
    inner = jnp.where(lanes <= plan.dims, inner, 0.0)
    every = jnp.where(lanes <= plan.dims, every, 0.0)
    for j in range(plan.gap_rows):
        moved = pltpu.roll(every, (plan.dims + 1 - plan.gap * j) % LANES, 1)
        turned[j] = jnp.where(lanes > plan.dims, moved, 0.0)
    row = iota(inner.shape, 0)

    def put(c, carry):
        mine = inner
        for q in range(plan.owned_pairs):
            for j in range(plan.gap_rows):
                pair = c * plan.owned_pairs + q
                piece = jnp.broadcast_to(turned[j, pl.ds(pair, 1), :], inner.shape)
                mine = mine + jnp.where(row == q * plan.gap_rows + j, piece, 0.0)
        for q in range(plan.cols):
            p = c * plan.cols + q
            send[p, 0 : plan.pairs] = mine
            send[p, plan.pairs : 2 * plan.pairs] = head
            send[p, 2 * plan.pairs :] = tail
        return carry

    repeat(plan.rows, put)


def correct_kernel(
    plan, starts, lam, got, ids, assign, moments, x_ref, out, centroids, a1, a2, stack, rows, spread
):
    k = plan.clusters
    offset = plan.offset()
    first, last = starts[plan.first_at], starts[plan.first_at + 1]
    segments = last - first + 1
    groups = lax.div(segments + plan.group - 1, plan.group)
    a1[...], a2[...] = split(assign[...])

    shape = (plan.devices, LANES)
    device = iota(shape, 0)

    def of(lane):
        return jnp.broadcast_to(ids[:, lane : lane + 1], shape)

    heads, tails = of(3 * k), of(3 * k + 1)
    head_ridge, tail_ridge = of(3 * k + 2), of(3 * k + 3)

    def shifted(value, distance):
        return pltpu.roll(value, distance % plan.devices, 0)

    links = []
    for hop in range(1, plan.reach + 1):
        before = device >= hop
        after = device < plan.devices - hop
        links.append(
            (
                hop,
                jnp.where(before & (shifted(tails, hop) == heads), 1.0, 0.0),
                jnp.where(after & (shifted(heads, -hop) == tails), 1.0, 0.0),
                jnp.where(before & (shifted(tails, hop) == tails), 1.0, 0.0),
                jnp.where(after & (shifted(tails, -hop) == tails), 1.0, 0.0),
            )
        )
    first_f, last_f = first.astype(f32), last.astype(f32)

    def gather(j, carry):
        inner = got[:, pl.ds(j, 1), :].reshape(shape)
        head = got[:, pl.ds(plan.pairs + j, 1), :].reshape(shape)
        tail = got[:, pl.ds(2 * plan.pairs + j, 1), :].reshape(shape)
        head_mass = halves(head, plan.dims)
        tail_mass = halves(tail, plan.dims)
        whole_head, whole_tail = head_mass, tail_mass
        for hop, back, ahead, same_back, same_ahead in links:
            whole_head = whole_head + back * shifted(tail_mass, hop)
            whole_tail = whole_tail + ahead * shifted(head_mass, -hop)
            whole_tail = whole_tail + same_back * shifted(tail_mass, hop)
            whole_tail = whole_tail + same_ahead * shifted(tail_mass, -hop)
        shrunk = head * (head_ridge / (whole_head + head_ridge))
        shrunk = shrunk + tail * (tail_ridge / (whole_tail + tail_ridge))
        right = jnp.sum(inner + shrunk, axis=0, keepdims=True)
        rows[0, pl.ds(j, 1)] = right / (1.0 + halves(right, plan.dims))
        for i, batch in ((1, first_f), (2, last_f)):
            both = jnp.where(heads == batch, head, 0.0) + jnp.where(tails == batch, tail, 0.0)
            rows[i, pl.ds(j, 1)] = jnp.sum(both, axis=0, keepdims=True)
        rows[3, pl.ds(j, 1)] = jnp.sum(inner, axis=0, keepdims=True)
        return carry

    repeat(plan.pairs, gather)

    lanes = lax.rem(iota((1, LANES), 1), HALF)
    for q in range(plan.owned_pairs):
        every = jnp.zeros((1, LANES), f32)
        for j in range(plan.gap_rows):
            at = q * plan.gap_rows + j
            piece = jnp.where(lanes > plan.dims, rows[3, at : at + 1], 0.0)
            moved = pltpu.roll(piece, (plan.gap * j - plan.dims - 1) % LANES, 1)
            inside = (lanes >= plan.gap * j) & (lanes < plan.gap * (j + 1))
            every = every + jnp.where(inside, moved, 0.0)
        every = every / (1.0 + halves(every, plan.dims))
        centroids[2 * q : 2 * q + 1] = every[:, 0 : plan.dims]
        centroids[2 * q + 1 : 2 * q + 2] = pltpu.roll(every, HALF, 1)[:, 0 : plan.dims]

    intercept = unpack_pairs(spread, rows[0])
    first_sum = unpack_pairs(spread, rows[1])
    last_sum = unpack_pairs(spread, rows[2])
    out[...] = x_ref[...]
    left = iota((k, LANES), 1) < HALF

    def apply(g, carry):
        masked(plan, a1, a2, stack, starts, offset, g)
        held = moments[pl.ds(pl.multiple_of(g * plan.depth, plan.depth), plan.depth), :]
        slopes = []
        for j in range(plan.group):
            s = g * plan.group + j
            part = held[j * k : (j + 1) * k]
            part = jnp.where(s == 0, first_sum, part)
            part = jnp.where(s == segments - 1, last_sum, part)
            mass = lane_of(part, plan.dims)
            ridge = lam[jnp.minimum(first + s, plan.batches - 1)]
            slope = (part - mass * intercept) / (mass + ridge)
            s1, s2 = split(slope)
            slopes.append(jnp.where(left, s1.astype(f32), s2.astype(f32)))
        slopes = jnp.concatenate(slopes, axis=0).astype(bf16)
        slopes = jnp.concatenate([slopes, slopes], axis=0)
        chunk = min(plan.cells, 1024)
        for c in range(plan.cells // chunk):
            at = slice(c * chunk, (c + 1) * chunk)
            moved = lax.dot_general(
                slopes, stack[:, at], (((0,), (0,)), ((), ())), preferred_element_type=f32
            )
            moved = moved[0:HALF] + moved[HALF:]
            out[:, at] = out[:, at] - moved[0 : plan.dims]
        return carry

    lax.fori_loop(0, groups, apply, 0)


def vmem():
    return pl.BlockSpec(memory_space=pltpu.VMEM)


def smem():
    return pl.BlockSpec(memory_space=pltpu.SMEM)


def shaped(shape, kind=f32):
    return jax.ShapeDtypeStruct(shape, kind)


def bound(kernel, plan, name):
    def run(*refs):
        kernel(plan, *refs)

    run.__name__ = name
    return run


def body(x, means, scale, lam, pop):
    plan = Plan(x, means, pop)
    k, cells = plan.clusters, plan.cells
    send, prior, counts, starts = pl.pallas_call(
        bound(count_kernel, plan, "count"),
        name="count",
        out_shape=(
            shaped((plan.devices, plan.width)),
            shaped((k, cells)),
            shaped((plan.blocks, k, LANES)),
            shaped((plan.table,), jnp.int32),
        ),
        in_specs=[smem(), smem(), smem(), vmem(), vmem()],
        out_specs=(vmem(), vmem(), vmem(), smem()),
        scratch_shapes=[pltpu.VMEM((HALF, cells), f32), pltpu.VMEM((k, LANES), f32)],
    )(pop, lam, scale, means, x)
    ids = lax.all_to_all(send, AXES, 0, 0, tiled=True)
    send, assign, moments = pl.pallas_call(
        bound(moment_kernel, plan, "moment"),
        name="moment",
        out_shape=(
            shaped((plan.devices, 3 * plan.pairs, LANES)),
            shaped((k, cells)),
            shaped((plan.groups * plan.depth, LANES)),
        ),
        in_specs=[smem(), smem(), vmem(), vmem(), vmem(), vmem()],
        out_specs=(vmem(), vmem(), vmem()),
        scratch_shapes=[
            pltpu.VMEM((HALF, cells), f32),
            pltpu.VMEM((k, cells), f32),
            pltpu.VMEM((k, cells), bf16),
            pltpu.VMEM((k, cells), bf16),
            pltpu.VMEM((2 * plan.depth, cells), bf16),
            pltpu.VMEM((4, k, LANES), f32),
            pltpu.VMEM((plan.gap_rows, plan.pairs, LANES), f32),
        ],
    )(starts, lam, ids, prior, counts, x)
    got = lax.all_to_all(send, AXES, 0, 0, tiled=True)
    corrected, centroids = pl.pallas_call(
        bound(correct_kernel, plan, "correct"),
        name="correct",
        out_shape=(shaped(x.shape), shaped((k // plan.rows, plan.dims))),
        in_specs=[smem(), smem(), vmem(), vmem(), vmem(), vmem(), vmem()],
        out_specs=(vmem(), vmem()),
        scratch_shapes=[
            pltpu.VMEM((k, cells), bf16),
            pltpu.VMEM((k, cells), bf16),
            pltpu.VMEM((2 * plan.depth, cells), bf16),
            pltpu.VMEM((4, plan.pairs, LANES), f32),
            pltpu.VMEM((k, LANES), f32),
        ],
    )(starts, lam, got, ids, assign, moments, x)
    return corrected, centroids


def solution(mesh):
    return jax.shard_map(
        body,
        mesh=mesh,
        in_specs=(P(None, AXES), P(), P(), P(), P()),
        out_specs=(P(None, AXES), P("cells", None)),
        check_vma=False,
    )
```

time: 230 us -> 45.3 us (0.20)
  the two profiles are of different devices: /device:TPU:28 before, /device:TPU:0 now
where the time goes in v1:
time: 45.3 us
  blocking collectives  31.4 us (69%)
  Pallas kernels  13.2 us (29%)
  between operations  0.64 us (1%)
    all_to_all x1, blocking collectives, body(): got = lax.all_to_all(send, AXES, 0, 0, tiled=True)  16.5 us
    all_to_all x1, blocking collectives, body(): ids = lax.all_to_all(send, AXES, 0, 0, tiled=True)  14.9 us
    pallas_call x1, Pallas kernels, body(): pl.pallas_call(bound(correct_kernel, plan, 'correct'), name='correct', ou...  5.53 us
    pallas_call x1, Pallas kernels, body(): pl.pallas_call(bound(moment_kernel, plan, 'moment'), name='moment', out_s...  4.35 us
    pallas_call x1, Pallas kernels, body(): pl.pallas_call(bound(count_kernel, plan, 'count'), name='count', out_shap...  3.36 us

profile of v1, /device:TPU:0, one launch (start us, length us, event | category | flops | bytes accessed | tf_op | source)
XLA Modules:
  0.0 45.3 jit_solution(16390693638695724515)
XLA Ops:
  0.6 3.4 %count.1 = (f32[32,128]{1,0:T(8,128)}, f32[16,4096]{1,0:T(8,128)}, f32[1,16,128]{2,1,0:T(8,128)}, s32[210]{0:T(256)}) custom-call(s32[200]{0:T(256)} %refs_0_.1, f32[200]{0:T(256)} %refs_1_.5, f32[16]{0:T(128)} %refs_2_.1, f32[16,50]{1,0:T(8,128)} %refs_3_.1, f32[50,4096]{1,0:T(8,128)} %refs_6_.1), custom_call_target="tpu_custom_call" | custom-call | tf_op jit(solution)/shard_map/count/pallas_call | solution.py:452
  4.0 14.9 %all_to_all.16 = f32[32,1,128]{2,1,0:T(1,128)} all-to-all(f32[32,1,128]{2,1,0:T(1,128)} %bitcast.6), channel_id=1, replica_groups=mesh['cells'=8,'grp'=4] {'cells','grp'}, dimensions={0} | all-to-all | bytes 32768 | tf_op jit(solution)/shard_map/all_to_all | solution.py:465
  18.9 4.3 %moment.1 = (f32[32,24,128]{2,1,0:T(8,128)}, f32[16,4096]{1,0:T(8,128)}, f32[1792,128]{1,0:T(8,128)}) custom-call(s32[210]{0:T(256)} %get-tuple-element.9.refs_0_, f32[200]{0:T(256)} %refs_1_.5, f32[32,128]{1,0:T(8,128)} %bitcast.4, f32[16,4096]{1,0:T(8,128)} %get-tuple-element.11.refs_3_, f32[1,16,128]{2,1,0:T(8,128)} %get-tuple-element.12.refs_4_, ...), custom_call_target="tpu_custom_call" | custom-call | tf_op jit(solution)/shard_map/moment/pallas_call | solution.py:466
  23.2 16.5 %all_to_all.17.refs_2_ = f32[32,24,128]{2,1,0:T(8,128)} all-to-all(f32[32,24,128]{2,1,0:T(8,128)} %get-tuple-element.13), channel_id=1, replica_groups=mesh['cells'=8,'grp'=4] {'cells','grp'}, dimensions={0} | all-to-all | bytes 786432 | tf_op jit(solution)/shard_map/all_to_all | solution.py:486
  39.7 5.5 %correct.1 = (f32[50,4096]{1,0:T(8,128)}, f32[2,50]{1,0:T(2,128)}) custom-call(s32[210]{0:T(256)} %get-tuple-element.9.refs_0_, f32[200]{0:T(256)} %refs_1_.5, f32[32,24,128]{2,1,0:T(8,128)} %all_to_all.17.refs_2_, f32[32,128]{1,0:T(8,128)} %bitcast.5, f32[16,4096]{1,0:T(8,128)} %get-tuple-element.14.refs_4_, f32[1792,128]{1,0:T(8,128)} %get-tuple-element.15.refs_5_, ...), custom_call_target="tpu_custom_call" | custom-call | tf_op jit(solution)/shard_map/correct/pallas_call | solution.py:487

commit v2 on v1

v2 whole, which is shorter than its diff:
```python
import jax
import jax.numpy as jnp
from jax import lax
from jax.experimental import pallas as pl
from jax.experimental.pallas import tpu as pltpu
from jax.sharding import PartitionSpec as P

f32 = jnp.float32
bf16 = jnp.bfloat16
i32 = jnp.int32
HALF = 64
LANES = 128
TILE = 16
AXES = ("cells", "grp")
BY_CELLS = (((1,), (1,)), ((), ()))
BY_ROWS = (((0,), (0,)), ((), ()))


def iota(shape, axis):
    return lax.broadcasted_iota(i32, shape, axis)


def split(value, parts):
    out = []
    for i in range(parts):
        out.append(value.astype(bf16))
        if i + 1 < parts:
            value = value - out[-1].astype(f32)
    return out


def lane_of(value, lane):
    return jnp.broadcast_to(value[:, lane : lane + 1], value.shape)


def halves(value, lane):
    left = iota(value.shape, 1) < HALF
    return jnp.where(left, lane_of(value, lane), lane_of(value, HALF + lane))


def column(row, first, count):
    shape = (count, row.shape[1])
    pick = iota(shape, 1) == iota(shape, 0) + first
    return jnp.sum(jnp.where(pick, jnp.broadcast_to(row, shape), 0.0), axis=1, keepdims=True)


def pack_pairs(ref):
    pairs = ref.shape[0] // 2
    even = ref[pl.ds(0, pairs, stride=2), :]
    odd = ref[pl.ds(1, pairs, stride=2), :]
    return jnp.where(iota(even.shape, 1) < HALF, even, odd)


def unpack_pairs(ref, tile):
    pairs = tile.shape[0]
    left = iota(tile.shape, 1) < HALF
    turned = pltpu.roll(tile, HALF, 1)
    ref[pl.ds(0, pairs, stride=2), :] = jnp.where(left, tile, turned)
    ref[pl.ds(1, pairs, stride=2), :] = jnp.where(left, turned, tile)
    return ref[...]


def repeat(count, step):
    if count <= 32:
        for i in range(count):
            step(i, 0)
    else:
        lax.fori_loop(0, count, step, 0)


class Plan:
    def __init__(self, x, means, pop):
        self.dims, self.cells = x.shape
        self.clusters = means.shape[0]
        self.batches = pop.shape[0]
        self.rows = lax.axis_size("cells")
        self.cols = lax.axis_size("grp")
        self.devices = self.rows * self.cols
        self.total = self.cells * self.devices
        self.most = 2 * self.total // self.batches
        self.reach = (self.most - 2) // self.cells + 1
        self.lone = self.most >= self.cells
        outside = -(-(self.total - self.cells) // self.most)
        local = min(self.batches, self.batches - outside + 2)
        self.tiles = -(-local // TILE)
        self.local = self.tiles * TILE
        self.group = max(1, LANES // self.clusters)
        self.groups = self.local // self.group
        self.depth = self.group * self.clusters
        self.width = -(-(3 * self.clusters + 4) // LANES) * LANES
        self.pairs = self.clusters // 2
        self.gap = HALF - (self.dims + 1)
        self.gap_rows = -(-(self.dims + 1) // self.gap)
        self.owned_pairs = self.clusters // self.rows // 2
        self.keep = self.devices * self.pairs * 3 * LANES * 4 <= 1 << 20
        self.chunk = min(self.cells, 1024)
        self.chunks = self.cells // self.chunk

    def at(self, c):
        return slice(c * self.chunk, (c + 1) * self.chunk)


def count_kernel(plan, pop, lam, scale, means, x_hbm, send, prior, counts, sizes, places, parts, xs, info, ridges, ends, ms, seg, sems):
    k = plan.clusters
    copies = [
        pltpu.make_async_copy(x_hbm.at[:, plan.at(c)], xs.at[:, plan.at(c)], sems.at[c])
        for c in range(plan.chunks)
    ]
    for copy in copies:
        copy.start()
    offset = (lax.axis_index("cells") * plan.cols + lax.axis_index("grp")) * plan.cells
    running, first, last = jnp.int32(0), jnp.int32(0), jnp.int32(0)
    for b in range(plan.batches):
        running = running + pop[b]
        ends[b] = running
        first = first + (running <= offset).astype(i32)
        last = last + (running <= offset + plan.cells - 1).astype(i32)
    segments = last - first + 1
    tiles = lax.div(segments + TILE - 1, TILE)
    info[0], info[1], info[2] = first, last, segments

    lane = iota((1, LANES), 1)
    cell = iota((8, plan.cells), 1)
    half = TILE // 2
    seg[...] = jnp.zeros_like(seg)

    def locate(g, carry):
        held = seg[...]
        for j in range(half):
            b = jnp.minimum(first + g * half + j, plan.batches - 1)
            held = held + jnp.where(cell >= ends[b] - offset, 1.0, 0.0)
        seg[...] = held
        return carry

    lax.fori_loop(0, lax.div(segments + half - 1, half), locate, 0)

    def note(g, carry):
        row = jnp.zeros((1, LANES), f32)
        for j in range(TILE):
            b = jnp.minimum(first + g * TILE + j, plan.batches - 1)
            ridges[g * TILE + j] = lam[b]
            row = jnp.where(lane == j, pop[b].astype(f32), row)
        sizes[pl.ds(g, 1), :] = row
        return carry

    lax.fori_loop(0, tiles, note, 0)

    ms[...] = jnp.zeros_like(ms)
    ms[:, 0 : plan.dims] = means[...]
    m = ms[...]
    m1, m2, m3 = [part.astype(f32) for part in split(m, 3)]
    zero = jnp.zeros_like(m)

    def twice(value):
        return value + pltpu.roll(value, HALF, 1)

    weights = jnp.concatenate(
        [
            jnp.concatenate([twice(m1), m1], axis=1),
            jnp.concatenate([twice(m2), zero], axis=1),
            jnp.concatenate([m3, zero], axis=1),
        ],
        axis=0,
    ).astype(bf16)
    lengths = jnp.sum(m * m, axis=1, keepdims=True)
    soft = jnp.ones((k, 1), f32)
    row = iota((k, 1), 0)
    for c in range(k):
        soft = jnp.where(row == c, scale[c], soft)
    inverse = 1.0 / (2.0 * soft)
    low = plan.dims // 8 * 8
    over = plan.dims - low
    shape = (8, plan.chunk)
    tail_row = iota(shape, 0)
    constant = jnp.where(tail_row == over, 1.0, 0.0)
    rest = [jnp.zeros(shape, f32)] * ((HALF - low) // 8 - 1)
    spots = iota((TILE, plan.chunk), 0).astype(f32).astype(bf16)
    found = jnp.zeros((3 * k, TILE), f32)
    for c in range(plan.chunks):
        at = plan.at(c)
        copies[c].wait()
        if over:
            moved = pltpu.roll(xs[plan.dims - 8 : plan.dims, at], over, 0)
            tail = jnp.where(tail_row < over, moved, constant)
        else:
            tail = constant
        x = jnp.concatenate([xs[0:low, at], tail] + rest, axis=0)
        x1, x2, x3 = split(x, 3)
        parts[0:HALF, at] = x1
        parts[HALF:, at] = x2
        stacked = jnp.concatenate([x1, x2, x3, jnp.zeros_like(x1)], axis=0)
        dots = jnp.dot(weights, stacked, preferred_element_type=f32)
        dots = dots[0:k] + dots[k : 2 * k] + dots[2 * k : 3 * k]
        scores = (2.0 * dots - lengths) * inverse
        raised = jnp.exp(scores - jnp.max(scores, axis=0, keepdims=True))
        chance = raised / jnp.sum(raised, axis=0, keepdims=True)
        prior[:, at] = chance
        place = jnp.concatenate([seg[:, at]] * (TILE // 8), axis=0).astype(bf16)
        places[:, at] = place
        hot = jnp.where(place == spots, bf16(1), bf16(0))
        found = found + lax.dot_general(
            jnp.concatenate(split(chance, 3), axis=0), hot, BY_CELLS, preferred_element_type=f32
        )

    def settle(g, found):
        found = found[0:k] + found[k : 2 * k] + found[2 * k :]
        counts[g] = jnp.concatenate([found, jnp.zeros((k, LANES - TILE), f32)], axis=1)

    settle(0, found)

    def count(g, carry):
        rows = (iota((TILE, plan.cells), 0) + g * TILE).astype(f32).astype(bf16)
        hot = jnp.where(places[...] == rows, bf16(1), bf16(0))
        settle(
            g,
            lax.dot_general(
                jnp.concatenate(split(prior[...], 3), axis=0), hot, BY_CELLS, preferred_element_type=f32
            ),
        )
        return carry

    lax.fori_loop(1, tiles, count, 0)

    every = lax.fori_loop(1, tiles, lambda g, total: total + counts[g], counts[0])
    total = jnp.sum(every, axis=1, keepdims=True)
    here = segments - 1
    end = counts[lax.div(here, TILE)]
    wide = iota((k, LANES), 1)
    last_count = jnp.sum(jnp.where(wide == lax.rem(here, TILE), end, 0.0), axis=1, keepdims=True)
    first_count = jnp.where(segments > 1, counts[0][:, 0:1], 0.0)
    spread = (k, plan.width)
    turn = iota(spread, 1) - iota(spread, 0)
    out = jnp.where(turn == 0, total, 0.0)
    out = jnp.where(turn == k, first_count, out)
    out = jnp.where(turn == 2 * k, last_count, out)
    out = jnp.sum(out, axis=0, keepdims=True)
    lanes = iota((1, plan.width), 1)
    out = jnp.where(lanes == 3 * k, first.astype(f32), out)
    out = jnp.where(lanes == 3 * k + 1, last.astype(f32), out)
    out = jnp.where(lanes == 3 * k + 2, lam[first], out)
    out = jnp.where(lanes == 3 * k + 3, lam[last], out)
    send[...] = jnp.broadcast_to(out, send.shape)


def masked(plan, a1, a2, places, g, at):
    k = plan.clusters
    width = at.stop - at.start
    shape = (TILE, width)
    base = jnp.full(shape, (g * plan.group).astype(f32) if not isinstance(g, int) else f32(g * plan.group))
    relative = places[:, at] - base.astype(bf16)
    out = []
    for a in (a1[:, at], a2[:, at]):
        for j in range(plan.group):
            inside = jnp.concatenate([relative] * (k // TILE), axis=0) == bf16(j)
            out.append(jnp.where(inside, a, bf16(0)))
    return jnp.concatenate(out, axis=0)


def moment_kernel(
    plan, info, ridges, got, prior, counts, sizes, places, parts, send, a1, a2, moments, wide, sums, turned
):
    k = plan.clusters
    first, last, segments = info[0], info[1], info[2]
    groups = lax.div(segments + plan.group - 1, plan.group)
    tiles = lax.div(segments + TILE - 1, TILE)

    table = got[...]
    total = column(jnp.sum(table, axis=0, keepdims=True), 0, k)
    heads, tails = table[:, 3 * k : 3 * k + 1], table[:, 3 * k + 1 : 3 * k + 2]

    def complete(batch):
        batch = batch.astype(f32)
        of_heads = jnp.sum(jnp.where(heads == batch, table, 0.0), axis=0, keepdims=True)
        of_tails = jnp.sum(jnp.where(tails == batch, table, 0.0), axis=0, keepdims=True)
        return column(of_heads, k, k) + column(of_tails, 2 * k, k)

    first_count, last_count = complete(first), complete(last)
    share = total / f32(plan.total)
    lane = iota((k, LANES), 1)

    def factors(g):
        held = counts[g]
        held = jnp.where(lane + g * TILE == 0, first_count, held)
        held = jnp.where(lane + g * TILE == segments - 1, last_count, held)
        ratio = (sizes[pl.ds(g, 1), :] * share + 1.0) / (held + 1.0)
        ratio = jnp.where(lane < TILE, ratio * ratio, 0.0)
        w1, w2, w3 = [part.astype(f32) for part in split(ratio, 3)]
        row = w1 + pltpu.roll(w2, TILE, 1) + pltpu.roll(w3, 2 * TILE, 1)
        return row.astype(bf16)[:, 0 : 4 * TILE]

    def factor_of(weights, g, at):
        shape = (TILE, at.stop - at.start)
        rows = (iota(shape, 0) + g * TILE).astype(f32).astype(bf16)
        hot = jnp.where(places[:, at] == rows, bf16(1), bf16(0))
        hot = jnp.concatenate([hot, hot, hot, jnp.zeros_like(hot)], axis=0)
        return jnp.dot(weights, hot, preferred_element_type=f32)

    weights = factors(0)
    for c in range(plan.chunks):
        wide[:, plan.at(c)] = factor_of(weights, 0, plan.at(c))

    def more(g, carry):
        weights = factors(g)
        for c in range(plan.chunks):
            wide[:, plan.at(c)] += factor_of(weights, g, plan.at(c))
        return carry

    lax.fori_loop(1, tiles, more, 0)
    for c in range(plan.chunks):
        at = plan.at(c)
        raised = prior[:, at] * wide[:, at]
        a1[:, at], a2[:, at] = split(raised / jnp.sum(raised, axis=0, keepdims=True), 2)

    sums[...] = jnp.zeros_like(sums)

    def gather(g, carry):
        both = jnp.zeros((2 * plan.depth, LANES), f32)
        for c in range(plan.chunks):
            at = plan.at(c)
            both = both + lax.dot_general(
                masked(plan, a1, a2, places, g, at), parts[:, at], BY_CELLS, preferred_element_type=f32
            )
        both = both[0 : plan.depth] + both[plan.depth :]
        both = both + pltpu.roll(both, HALF, 1)
        moments[pl.ds(pl.multiple_of(g * plan.depth, plan.depth), plan.depth), :] = both
        mass = lane_of(both, plan.dims)
        inner, head, tail, every = sums[0], sums[1], sums[2], sums[3]
        for j in range(plan.group):
            s = g * plan.group + j
            at = slice(j * k, (j + 1) * k)
            ridge = ridges[s]
            part = both[at]
            every = every + part
            shrunk = part * (ridge / (mass[at] + ridge))
            inner = inner + jnp.where((s > 0) & (s < segments - 1), shrunk, 0.0)
            head = head + jnp.where((s == 0) & (segments > 1), part, 0.0)
            tail = tail + jnp.where(s == segments - 1, part, 0.0)
        sums[0], sums[1], sums[2], sums[3] = inner, head, tail, every
        return carry

    lax.fori_loop(0, groups, gather, 0)
    inner, head, tail, every = [pack_pairs(sums.at[i]) for i in range(4)]
    lanes = lax.rem(iota(inner.shape, 1), HALF)
    inner = jnp.where(lanes <= plan.dims, inner, 0.0)
    every = jnp.where(lanes <= plan.dims, every, 0.0)
    for j in range(plan.gap_rows):
        moved = pltpu.roll(every, (plan.dims + 1 - plan.gap * j) % LANES, 1)
        turned[j] = jnp.where(lanes > plan.dims, moved, 0.0)
    row = iota(inner.shape, 0)

    def put(c, carry):
        mine = inner
        for q in range(plan.owned_pairs):
            for j in range(plan.gap_rows):
                pair = c * plan.owned_pairs + q
                piece = jnp.broadcast_to(turned[j, pl.ds(pair, 1), :], inner.shape)
                mine = mine + jnp.where(row == q * plan.gap_rows + j, piece, 0.0)
        for q in range(plan.cols):
            p = c * plan.cols + q
            send[p, 0 : plan.pairs] = mine
            send[p, plan.pairs : 2 * plan.pairs] = head
            send[p, 2 * plan.pairs :] = tail
        return carry

    repeat(plan.rows, put)


def correct_kernel(
    plan, info, ridges, got, ids, a1, a2, moments, places, xs, out_hbm, centroids, marks, slopes, rows, spread, out, sems
):
    k = plan.clusters
    first, last, segments = info[0], info[1], info[2]
    groups = lax.div(segments + plan.group - 1, plan.group)
    shape = (plan.devices, LANES)
    device = iota(shape, 0)

    def of(lane):
        return jnp.broadcast_to(ids[:, lane : lane + 1], shape)

    heads, tails = of(3 * k), of(3 * k + 1)
    first_f, last_f = first.astype(f32), last.astype(f32)

    def shifted(value, distance):
        return pltpu.roll(value, distance % plan.devices, 0)

    marks[0], marks[1] = of(3 * k + 2), of(3 * k + 3)
    for i, (side, batch) in enumerate(
        ((heads, first_f), (tails, first_f), (heads, last_f), (tails, last_f))
    ):
        marks[2 + i] = jnp.where(side == batch, 1.0, 0.0)
    links = []

    def link(hop, mine, theirs, into, source):
        inside = (device + hop >= 0) & (device + hop < plan.devices)
        at = 6 + len(links)
        marks[at] = jnp.where(inside & (shifted(theirs, -hop) == mine), 1.0, 0.0)
        links.append((at, hop, into, source))

    for hop in range(1, plan.reach + 1):
        link(-hop, heads, tails, 0, 1)
        link(hop, tails, heads, 1, 0)
        if plan.lone:
            link(-hop, tails, tails, 1, 1)
            link(hop, tails, tails, 1, 1)

    p = plan.pairs
    block = (p, LANES)

    def mark(i, r):
        return jnp.broadcast_to(marks[i, pl.ds(r, 1), :], block)

    def side_of(r, side):
        return got[r, (1 + side) * p : (2 + side) * p]

    def gather(r, carry):
        right, inner, first_sum, last_sum = carry
        sides = [side_of(r, 0), side_of(r, 1)]
        whole = [halves(side, plan.dims) for side in sides]
        for at, hop, into, source in links:
            if isinstance(r, int):
                if not 0 <= r + hop < plan.devices:
                    continue
                other = r + hop
            else:
                other = jnp.clip(r + hop, 0, plan.devices - 1)
            whole[into] = whole[into] + mark(at, r) * halves(side_of(other, source), plan.dims)
        mine = got[r, 0:p]
        inner = inner + mine
        right = right + mine
        for i in range(2):
            ridge = mark(i, r)
            right = right + sides[i] * (ridge / (whole[i] + ridge))
            first_sum = first_sum + sides[i] * mark(2 + i, r)
            last_sum = last_sum + sides[i] * mark(4 + i, r)
        return right, inner, first_sum, last_sum

    state = (jnp.zeros(block, f32),) * 4
    if plan.devices <= 32:
        for r in range(plan.devices):
            state = gather(r, state)
    else:
        state = lax.fori_loop(0, plan.devices, gather, state)
    right, inner, first_sum, last_sum = state
    intercept = unpack_pairs(spread, right / (1.0 + halves(right, plan.dims)))
    first_sum = unpack_pairs(spread, first_sum)
    last_sum = unpack_pairs(spread, last_sum)
    left = iota((k, LANES), 1) < HALF

    def slope(g, carry):
        start = pl.multiple_of(g * plan.depth, plan.depth)
        held = moments[pl.ds(start, plan.depth), :]
        made = []
        for j in range(plan.group):
            s = g * plan.group + j
            part = held[j * k : (j + 1) * k]
            part = jnp.where(s == 0, first_sum, part)
            part = jnp.where(s == segments - 1, last_sum, part)
            mass = lane_of(part, plan.dims)
            ridge = ridges[s]
            s1, s2 = split((part - mass * intercept) / (mass + ridge), 2)
            made.append(jnp.where(left, s1.astype(f32), s2.astype(f32)))
        slopes[g] = jnp.transpose(jnp.concatenate(made, axis=0)).astype(bf16)
        return carry

    lax.fori_loop(0, groups, slope, 0)

    def move(g, at):
        mine = slopes[g]
        moved = jnp.dot(
            jnp.concatenate([mine, mine], axis=1),
            masked(plan, a1, a2, places, g, at),
            preferred_element_type=f32,
        )
        return (moved[0:HALF] + moved[HALF:])[0 : plan.dims]

    copies = []
    for c in range(plan.chunks):
        at = plan.at(c)
        out[:, at] = xs[:, at]

        def again(g, carry):
            out[:, at] = out[:, at] - move(g, at)
            return carry

        lax.fori_loop(0, groups, again, 0)
        copies.append(pltpu.make_async_copy(out.at[:, at], out_hbm.at[:, at], sems.at[c]))
        copies[-1].start()

    rows[...] = inner
    lanes = lax.rem(iota((1, LANES), 1), HALF)
    for q in range(plan.owned_pairs):
        every = jnp.zeros((1, LANES), f32)
        for j in range(plan.gap_rows):
            at = q * plan.gap_rows + j
            piece = jnp.where(lanes > plan.dims, rows[at : at + 1], 0.0)
            moved = pltpu.roll(piece, (plan.gap * j - plan.dims - 1) % LANES, 1)
            inside = (lanes >= plan.gap * j) & (lanes < plan.gap * (j + 1))
            every = every + jnp.where(inside, moved, 0.0)
        every = every / (1.0 + halves(every, plan.dims))
        centroids[2 * q : 2 * q + 1] = every[:, 0 : plan.dims]
        centroids[2 * q + 1 : 2 * q + 2] = pltpu.roll(every, HALF, 1)[:, 0 : plan.dims]
    for copy in copies:
        copy.wait()


VMEM = pl.BlockSpec(memory_space=pltpu.VMEM)
SMEM = pl.BlockSpec(memory_space=pltpu.SMEM)
WHERE = pl.BlockSpec(memory_space=pltpu.HBM)


def hold_scalars(value):
    return pltpu.with_memory_space_constraint(value, pltpu.SMEM)


def bound(kernel, plan, name):
    def run(*refs):
        kernel(plan, *refs)

    run.__name__ = name
    return run


def body(x, means, scale, lam, pop):
    plan = Plan(x, means, pop)
    k, cells = plan.clusters, plan.cells
    params = pltpu.CompilerParams(vmem_limit_bytes=(16 << 20) if plan.keep else None)

    def kept(shape, kind=f32):
        return pltpu.VMEM(shape, kind) if plan.keep else jax.ShapeDtypeStruct(shape, kind)

    def hold(value):
        return pltpu.with_memory_space_constraint(value, pltpu.VMEM) if plan.keep else value

    send, prior, counts, sizes, places, parts, xs, info, ridges = pl.pallas_call(
        bound(count_kernel, plan, "count"),
        name="count",
        out_shape=(
            kept((plan.devices, plan.width)),
            kept((k, cells)),
            kept((plan.tiles, k, LANES)),
            kept((plan.tiles, LANES)),
            kept((TILE, cells), bf16),
            kept((2 * HALF, cells), bf16),
            kept((plan.dims, cells)),
            pltpu.SMEM((4,), i32),
            pltpu.SMEM((plan.local,), f32),
        ),
        in_specs=[SMEM, SMEM, SMEM, VMEM, WHERE],
        out_specs=(VMEM,) * 7 + (SMEM,) * 2,
        scratch_shapes=[
            pltpu.SMEM((plan.batches,), i32),
            pltpu.VMEM((k, LANES), f32),
            pltpu.VMEM((8, cells), f32),
            pltpu.SemaphoreType.DMA((plan.chunks,)),
        ],
    )(pop, lam, scale, means, x)
    prior, counts, sizes, places, parts, xs = map(hold, (prior, counts, sizes, places, parts, xs))
    info, ridges = hold_scalars(info), hold_scalars(ridges)
    ids = hold(lax.all_to_all(send, AXES, 0, 0, tiled=True))
    send, a1, a2, moments = pl.pallas_call(
        bound(moment_kernel, plan, "moment"),
        name="moment",
        compiler_params=params,
        out_shape=(
            kept((plan.devices, 3 * plan.pairs, LANES)),
            kept((k, cells), bf16),
            kept((k, cells), bf16),
            kept((plan.groups * plan.depth, LANES)),
        ),
        in_specs=[SMEM] * 2 + [VMEM] * 6,
        out_specs=(VMEM,) * 4,
        scratch_shapes=[
            pltpu.VMEM((k, cells), f32),
            pltpu.VMEM((4, k, LANES), f32),
            pltpu.VMEM((plan.gap_rows, plan.pairs, LANES), f32),
        ],
    )(info, ridges, ids, prior, counts, sizes, places, parts)
    a1, a2, moments = map(hold, (a1, a2, moments))
    got = hold(lax.all_to_all(send, AXES, 0, 0, tiled=True))
    marks = 6 + plan.reach * (4 if plan.lone else 2)
    corrected, centroids = pl.pallas_call(
        bound(correct_kernel, plan, "correct"),
        name="correct",
        compiler_params=params,
        out_shape=(
            jax.ShapeDtypeStruct(x.shape, f32),
            jax.ShapeDtypeStruct((k // plan.rows, plan.dims), f32),
        ),
        in_specs=[SMEM] * 2 + [VMEM] * 7,
        out_specs=(WHERE, VMEM),
        scratch_shapes=[
            pltpu.VMEM((marks, plan.devices, LANES), f32),
            pltpu.VMEM((plan.groups, LANES, plan.depth), bf16),
            pltpu.VMEM((plan.pairs, LANES), f32),
            pltpu.VMEM((k, LANES), f32),
            pltpu.VMEM((plan.dims, cells), f32),
            pltpu.SemaphoreType.DMA((plan.chunks,)),
        ],
    )(info, ridges, got, ids, a1, a2, moments, places, xs)
    return corrected, centroids


def solution(mesh):
    return jax.shard_map(
        body,
        mesh=mesh,
        in_specs=(P(None, AXES), P(), P(), P(), P()),
        out_specs=(P(None, AXES), P("cells", None)),
        check_vma=False,
    )
```

time: 45.3 us -> 38.7 us (0.85); the launches traced: 45.3 us -> 39.5 us
  Pallas kernels: 13.2 us -> 9.58 us
  blocking collectives: 31.4 us -> 29.3 us
    pallas_call x2, Pallas kernels: 9.88 us -> 6.45 us  [the longest x1 4.11 us: body(): pl.pallas_call(bound(correct_kernel, plan, 'correct'), name='correct', co...]
    all_to_all x2, blocking collectives: 31.4 us -> 29.3 us  [the longest x1 15 us: body(): got = hold(lax.all_to_all(send, AXES, 0, 0, tiled=True))]
where the time goes in v2:
time: 38.7 us; the launch traced here: 39.5 us
  blocking collectives  29.3 us (76%)
  Pallas kernels  9.58 us (25%)
  between operations  0.64 us (2%)
    all_to_all x1, blocking collectives, body(): got = hold(lax.all_to_all(send, AXES, 0, 0, tiled=True))  15 us
    all_to_all x1, blocking collectives, body(): ids = hold(lax.all_to_all(send, AXES, 0, 0, tiled=True))  14.3 us
    pallas_call x1, Pallas kernels, body(): pl.pallas_call(bound(correct_kernel, plan, 'correct'), name='correct', co...  4.11 us
    pallas_call x1, Pallas kernels, body(): pl.pallas_call(bound(count_kernel, plan, 'count'), name='count', out_shap...  3.13 us
    pallas_call x1, Pallas kernels, body(): pl.pallas_call(bound(moment_kernel, plan, 'moment'), name='moment', compi...  2.33 us

profile of v2, /device:TPU:0, one launch (start us, length us, event | category | flops | bytes accessed | tf_op | source)
XLA Modules:
  0.0 39.5 jit_solution(12528267777093526987)
XLA Ops:
  0.6 3.1 %count.1 = (f32[32,128]{1,0:T(8,128)S(1)}, f32[16,4096]{1,0:T(8,128)S(1)}, f32[7,16,128]{2,1,0:T(8,128)S(1)}, f32[7,128]{1,0:T(8,128)S(1)}, bf16[16,4096]{1,0:T(...) custom-call(s32[200]{0:T(256)} %refs_0_.1, ...), custom_call_target="tpu_custom_call" | custom-call | tf_op jit(solution)/shard_map/count/pallas_call | solution.py:534
  3.8 14.3 %all_to_all.16 = f32[32,1,128]{2,1,0:T(1,128)S(1)} all-to-all(f32[32,1,128]{2,1,0:T(1,128)S(1)} %bitcast.6), channel_id=1, replica_groups=mesh['cells'=8,'grp'=4] {'cells','grp'}, dimensions={0} | all-to-all | bytes 32768 | tf_op jit(solution)/shard_map/all_to_all | solution.py:559
  18.1 2.3 %moment.1 = (f32[32,24,128]{2,1,0:T(8,128)S(1)}, bf16[16,4096]{1,0:T(8,128)(2,1)S(1)}, bf16[16,4096]{1,0:T(8,128)(2,1)S(1)}, f32[1792,128]{1,0:T(8,128)S(1)}) custom-call(s32[4]{0:T(128)S(4)} %get-tuple-element.15.refs_0_, f32[112]{0:T(128)S(4)} %get-tuple-element.16.refs_1_, f32[32,128]{1,0:T(8,128)S(1)} %bitcast.4, ...), custom_call_target="tpu_custom_call" | custom-call | tf_op jit(solution)/shard_map/moment/pallas_call | solution.py:560
  20.4 15.0 %all_to_all.17.refs_2_ = f32[32,24,128]{2,1,0:T(8,128)S(1)} all-to-all(f32[32,24,128]{2,1,0:T(8,128)S(1)} %get-tuple-element.23), channel_id=1, replica_groups=mesh['cells'=8,'grp'=4] {'cells','grp'}, dimensions={0} | all-to-all | bytes 786432 | tf_op jit(solution)/shard_map/all_to_all | solution.py:579
  35.4 4.1 %correct.1 = (f32[50,4096]{1,0:T(8,128)}, f32[2,50]{1,0:T(2,128)}) custom-call(s32[4]{0:T(128)S(4)} %get-tuple-element.15.refs_0_, f32[112]{0:T(128)S(4)} %get-tuple-element.16.refs_1_, f32[32,24,128]{2,1,0:T(8,128)S(1)} %all_to_all.17.refs_2_, f32[32,128]{1,0:T(8,128)S(1)} %bitcast.5, bf16[16,4096]{1,0:T(8,128)(2,1)S(1)} %get-tuple-element.24.refs_4_, ...), custom_call_target="tpu_custom_call" | custom-call | tf_op jit(solution)/shard_map/correct/pallas_call | solution.py:581

commit v3 on v2

--- a/solution.py
+++ b/solution.py
@@ -89,10 +89,12 @@
         self.depth = self.group * self.clusters
         self.width = -(-(3 * self.clusters + 4) // LANES) * LANES
         self.pairs = self.clusters // 2
+        self.part = self.pairs // 2
         self.gap = HALF - (self.dims + 1)
         self.gap_rows = -(-(self.dims + 1) // self.gap)
         self.owned_pairs = self.clusters // self.rows // 2
         self.keep = self.devices * self.pairs * 3 * LANES * 4 <= 1 << 20
+        self.fixed_marks = 10
         self.chunk = min(self.cells, 1024)
         self.chunks = self.cells // self.chunk
 
@@ -100,50 +102,32 @@
         return slice(c * self.chunk, (c + 1) * self.chunk)
 
 
-def count_kernel(plan, pop, lam, scale, means, x_hbm, send, prior, counts, sizes, places, parts, xs, info, ridges, ends, ms, seg, sems):
+def count_kernel(
+    plan, pop_hbm, lam_hbm, scale_hbm, means_hbm, x_hbm, send, prior, counts, sizes, places, parts, xs, info, ridges,
+    pop, lam, scale, means, ends, ms, seg, sems, small,
+):
     k = plan.clusters
+    inputs = [
+        pltpu.make_async_copy(source, target, small.at[i])
+        for i, (source, target) in enumerate(
+            ((pop_hbm, pop), (means_hbm, means), (scale_hbm, scale), (lam_hbm, lam))
+        )
+    ]
     copies = [
         pltpu.make_async_copy(x_hbm.at[:, plan.at(c)], xs.at[:, plan.at(c)], sems.at[c])
         for c in range(plan.chunks)
     ]
-    for copy in copies:
+    for copy in inputs + copies:
         copy.start()
     offset = (lax.axis_index("cells") * plan.cols + lax.axis_index("grp")) * plan.cells
-    running, first, last = jnp.int32(0), jnp.int32(0), jnp.int32(0)
+    for copy in inputs:
+        copy.wait()
+    copies[0].wait()
+    running, first = jnp.int32(0), jnp.int32(0)
     for b in range(plan.batches):
         running = running + pop[b]
         ends[b] = running
         first = first + (running <= offset).astype(i32)
-        last = last + (running <= offset + plan.cells - 1).astype(i32)
-    segments = last - first + 1
-    tiles = lax.div(segments + TILE - 1, TILE)
-    info[0], info[1], info[2] = first, last, segments
-
-    lane = iota((1, LANES), 1)
-    cell = iota((8, plan.cells), 1)
-    half = TILE // 2
-    seg[...] = jnp.zeros_like(seg)
-
-    def locate(g, carry):
-        held = seg[...]
-        for j in range(half):
-            b = jnp.minimum(first + g * half + j, plan.batches - 1)
-            held = held + jnp.where(cell >= ends[b] - offset, 1.0, 0.0)
-        seg[...] = held
-        return carry
-
-    lax.fori_loop(0, lax.div(segments + half - 1, half), locate, 0)
-
-    def note(g, carry):
-        row = jnp.zeros((1, LANES), f32)
-        for j in range(TILE):
-            b = jnp.minimum(first + g * TILE + j, plan.batches - 1)
-            ridges[g * TILE + j] = lam[b]
-            row = jnp.where(lane == j, pop[b].astype(f32), row)
-        sizes[pl.ds(g, 1), :] = row
-        return carry
-
-    lax.fori_loop(0, tiles, note, 0)
 
     ms[...] = jnp.zeros_like(ms)
     ms[:, 0 : plan.dims] = means[...]
@@ -174,11 +158,10 @@
     tail_row = iota(shape, 0)
     constant = jnp.where(tail_row == over, 1.0, 0.0)
     rest = [jnp.zeros(shape, f32)] * ((HALF - low) // 8 - 1)
-    spots = iota((TILE, plan.chunk), 0).astype(f32).astype(bf16)
-    found = jnp.zeros((3 * k, TILE), f32)
     for c in range(plan.chunks):
         at = plan.at(c)
-        copies[c].wait()
+        if c:
+            copies[c].wait()
         if over:
             moved = pltpu.roll(xs[plan.dims - 8 : plan.dims, at], over, 0)
             tail = jnp.where(tail_row < over, moved, constant)
@@ -195,18 +178,48 @@
         raised = jnp.exp(scores - jnp.max(scores, axis=0, keepdims=True))
         chance = raised / jnp.sum(raised, axis=0, keepdims=True)
         prior[:, at] = chance
-        place = jnp.concatenate([seg[:, at]] * (TILE // 8), axis=0).astype(bf16)
-        places[:, at] = place
-        hot = jnp.where(place == spots, bf16(1), bf16(0))
-        found = found + lax.dot_general(
-            jnp.concatenate(split(chance, 3), axis=0), hot, BY_CELLS, preferred_element_type=f32
-        )
+
+    def following(held):
+        return held[0] + 1, ends[held[0] + 1]
+
+    last, unused = lax.while_loop(
+        lambda held: held[1] < offset + plan.cells, following, (first, ends[first])
+    )
+    segments = last - first + 1
+    tiles = lax.div(segments + TILE - 1, TILE)
+    info[0], info[1], info[2] = first, last, segments
+
+    lane = iota((1, LANES), 1)
+    cell = iota((8, plan.cells), 1)
+    half = TILE // 2
+    seg[...] = jnp.zeros_like(seg)
+
+    def locate(g, carry):
+        held = seg[...]
+        for j in range(half):
+            s = g * half + j
+            b = jnp.minimum(first + s, plan.batches - 1)
+            held = jnp.where(cell >= ends[b] - offset, (s + 1).astype(f32), held)
+        seg[...] = held
+        return carry
+
+    lax.fori_loop(0, lax.div(segments + half - 1, half), locate, 0)
+    places[...] = jnp.concatenate([seg[...]] * (TILE // 8), axis=0).astype(bf16)
+
+    def note(g, carry):
+        row = jnp.zeros((1, LANES), f32)
+        for j in range(TILE):
+            b = jnp.minimum(first + g * TILE + j, plan.batches - 1)
+            ridges[g * TILE + j] = lam[b]
+            row = jnp.where(lane == j, pop[b].astype(f32), row)
+        sizes[pl.ds(g, 1), :] = row
+        return carry
+
+    lax.fori_loop(0, tiles, note, 0)
 
     def settle(g, found):
         found = found[0:k] + found[k : 2 * k] + found[2 * k :]
         counts[g] = jnp.concatenate([found, jnp.zeros((k, LANES - TILE), f32)], axis=1)
-
-    settle(0, found)
 
     def count(g, carry):
         rows = (iota((TILE, plan.cells), 0) + g * TILE).astype(f32).astype(bf16)
@@ -219,7 +232,7 @@
         )
         return carry
 
-    lax.fori_loop(1, tiles, count, 0)
+    lax.fori_loop(0, tiles, count, 0)
 
     every = lax.fori_loop(1, tiles, lambda g, total: total + counts[g], counts[0])
     total = jnp.sum(every, axis=1, keepdims=True)
@@ -346,31 +359,38 @@
     for j in range(plan.gap_rows):
         moved = pltpu.roll(every, (plan.dims + 1 - plan.gap * j) % LANES, 1)
         turned[j] = jnp.where(lanes > plan.dims, moved, 0.0)
-    row = iota(inner.shape, 0)
+    row = iota((plan.part, LANES), 0)
 
     def put(c, carry):
-        mine = inner
+        gaps = jnp.zeros((plan.part, LANES), f32)
         for q in range(plan.owned_pairs):
             for j in range(plan.gap_rows):
                 pair = c * plan.owned_pairs + q
-                piece = jnp.broadcast_to(turned[j, pl.ds(pair, 1), :], inner.shape)
-                mine = mine + jnp.where(row == q * plan.gap_rows + j, piece, 0.0)
+                piece = jnp.broadcast_to(turned[j, pl.ds(pair, 1), :], gaps.shape)
+                gaps = gaps + jnp.where(row == q * plan.gap_rows + j, piece, 0.0)
         for q in range(plan.cols):
             p = c * plan.cols + q
-            send[p, 0 : plan.pairs] = mine
-            send[p, plan.pairs : 2 * plan.pairs] = head
-            send[p, 2 * plan.pairs :] = tail
+            for side in range(2):
+                low = side * plan.part
+
+                def write(low=low, p=p):
+                    start = p * 3 * plan.part
+                    send[pl.ds(start, plan.part), :] = inner[low : low + plan.part] + gaps
+                    send[pl.ds(start + plan.part, plan.part), :] = head[low : low + plan.part]
+                    send[pl.ds(start + 2 * plan.part, plan.part), :] = tail[low : low + plan.part]
+
+                if isinstance(p, int):
+                    if p % 2 == side:
+                        write()
+                else:
+                    pl.when(lax.rem(p, 2) == side)(write)
         return carry
 
     repeat(plan.rows, put)
 
 
-def correct_kernel(
-    plan, info, ridges, got, ids, a1, a2, moments, places, xs, out_hbm, centroids, marks, slopes, rows, spread, out, sems
-):
-    k = plan.clusters
-    first, last, segments = info[0], info[1], info[2]
-    groups = lax.div(segments + plan.group - 1, plan.group)
+def reduce_kernel(plan, info, got, ids, mine, theirs, marks):
+    k, part = plan.clusters, plan.part
     shape = (plan.devices, LANES)
     device = iota(shape, 0)
 
@@ -378,72 +398,110 @@
         return jnp.broadcast_to(ids[:, lane : lane + 1], shape)
 
     heads, tails = of(3 * k), of(3 * k + 1)
-    first_f, last_f = first.astype(f32), last.astype(f32)
+    me = lax.axis_index("cells") * plan.cols + lax.axis_index("grp")
+    other = me + 1 - 2 * lax.rem(me, 2)
 
     def shifted(value, distance):
         return pltpu.roll(value, distance % plan.devices, 0)
 
     marks[0], marks[1] = of(3 * k + 2), of(3 * k + 3)
-    for i, (side, batch) in enumerate(
-        ((heads, first_f), (tails, first_f), (heads, last_f), (tails, last_f))
-    ):
-        marks[2 + i] = jnp.where(side == batch, 1.0, 0.0)
+    own = ids[pl.ds(me, 1), :]
+    pair = ids[pl.ds(other, 1), :]
+    for i, (row, lane) in enumerate(((own, 3 * k), (own, 3 * k + 1), (pair, 3 * k), (pair, 3 * k + 1))):
+        batch = jnp.broadcast_to(row[:, lane : lane + 1], shape)
+        marks[2 + 2 * i] = jnp.where(heads == batch, 1.0, 0.0)
+        marks[3 + 2 * i] = jnp.where(tails == batch, 1.0, 0.0)
     links = []
 
-    def link(hop, mine, theirs, into, source):
+    def link(hop, to_head, from_head, mine, theirs):
         inside = (device + hop >= 0) & (device + hop < plan.devices)
-        at = 6 + len(links)
+        at = plan.fixed_marks + len(links)
         marks[at] = jnp.where(inside & (shifted(theirs, -hop) == mine), 1.0, 0.0)
-        links.append((at, hop, into, source))
+        links.append((at, hop, to_head, from_head))
 
     for hop in range(1, plan.reach + 1):
-        link(-hop, heads, tails, 0, 1)
-        link(hop, tails, heads, 1, 0)
+        link(-hop, True, False, heads, tails)
+        link(hop, False, True, tails, heads)
         if plan.lone:
-            link(-hop, tails, tails, 1, 1)
-            link(hop, tails, tails, 1, 1)
-
-    p = plan.pairs
-    block = (p, LANES)
+            link(-hop, False, False, tails, tails)
+            link(hop, False, False, tails, tails)
+
+    block = (2 * part, LANES)
+    top = iota(block, 0) < part
 
     def mark(i, r):
         return jnp.broadcast_to(marks[i, pl.ds(r, 1), :], block)
 
-    def side_of(r, side):
-        return got[r, (1 + side) * p : (2 + side) * p]
+    def two(i, r):
+        return jnp.where(top, mark(i, r), mark(i + 1, r))
+
+    def ends_of(r):
+        return got[pl.ds(r * 3 * part + part, 2 * part), :]
+
+    def turn(value):
+        return pltpu.roll(value, part, 0)
 
     def gather(r, carry):
-        right, inner, first_sum, last_sum = carry
-        sides = [side_of(r, 0), side_of(r, 1)]
-        whole = [halves(side, plan.dims) for side in sides]
-        for at, hop, into, source in links:
+        inner, shrunk, sums = carry
+        ends = ends_of(r)
+        whole = halves(ends, plan.dims)
+        for at, hop, to_head, from_head in links:
             if isinstance(r, int):
                 if not 0 <= r + hop < plan.devices:
                     continue
-                other = r + hop
+                there = r + hop
             else:
-                other = jnp.clip(r + hop, 0, plan.devices - 1)
-            whole[into] = whole[into] + mark(at, r) * halves(side_of(other, source), plan.dims)
-        mine = got[r, 0:p]
-        inner = inner + mine
-        right = right + mine
-        for i in range(2):
-            ridge = mark(i, r)
-            right = right + sides[i] * (ridge / (whole[i] + ridge))
-            first_sum = first_sum + sides[i] * mark(2 + i, r)
-            last_sum = last_sum + sides[i] * mark(4 + i, r)
-        return right, inner, first_sum, last_sum
-
-    state = (jnp.zeros(block, f32),) * 4
+                there = jnp.clip(r + hop, 0, plan.devices - 1)
+            mass = halves(ends_of(there), plan.dims)
+            if to_head != from_head:
+                mass = turn(mass)
+            whole = whole + jnp.where(top == to_head, mark(at, r) * mass, 0.0)
+        ridge = two(0, r)
+        shrunk = shrunk + ends * (ridge / (whole + ridge))
+        inner = inner + got[pl.ds(r * 3 * part, part), :]
+        sums = tuple(total + ends * two(2 + 2 * i, r) for i, total in enumerate(sums))
+        return inner, shrunk, sums
+
+    zero = jnp.zeros(block, f32)
+    state = (zero[0:part], zero, (zero,) * 4)
     if plan.devices <= 32:
         for r in range(plan.devices):
             state = gather(r, state)
     else:
         state = lax.fori_loop(0, plan.devices, gather, state)
-    right, inner, first_sum, last_sum = state
-    intercept = unpack_pairs(spread, right / (1.0 + halves(right, plan.dims)))
-    first_sum = unpack_pairs(spread, first_sum)
-    last_sum = unpack_pairs(spread, last_sum)
+    inner, shrunk, sums = state
+
+    def fold(value):
+        return (value + turn(value))[0:part]
+
+    right = inner + fold(shrunk)
+    intercept = right / (1.0 + halves(right, plan.dims))
+    mine[0] = jnp.concatenate([intercept, intercept], axis=0)
+    theirs[0:part] = intercept
+    for i in range(2):
+        value = sums[i] + turn(sums[i])
+        mine[1 + i] = value
+        theirs[(1 + i) * part : (2 + i) * part] = fold(sums[2 + i])
+    mine[3] = jnp.concatenate([inner, inner], axis=0)
+
+
+def correct_kernel(
+    plan, info, ridges, mine, theirs, a1, a2, moments, places, xs, out_hbm, centroids_hbm,
+    slopes, rows, spread, out, centroids, sems, done,
+):
+    k, part = plan.clusters, plan.part
+    first, last, segments = info[0], info[1], info[2]
+    groups = lax.div(segments + plan.group - 1, plan.group)
+    me = lax.axis_index("cells") * plan.cols + lax.axis_index("grp")
+    odd = jnp.full((plan.pairs, LANES), lax.rem(me, 2)) == 1
+    low = iota((plan.pairs, LANES), 0) < part
+
+    def both(i):
+        piece = theirs[i * part : (i + 1) * part]
+        piece = jnp.concatenate([piece, piece], axis=0)
+        return unpack_pairs(spread, jnp.where(low != odd, mine[i], piece))
+
+    intercept, first_sum, last_sum = both(0), both(1), both(2)
     left = iota((k, LANES), 1) < HALF
 
     def slope(g, carry):
@@ -473,20 +531,7 @@
         )
         return (moved[0:HALF] + moved[HALF:])[0 : plan.dims]
 
-    copies = []
-    for c in range(plan.chunks):
-        at = plan.at(c)
-        out[:, at] = xs[:, at]
-
-        def again(g, carry):
-            out[:, at] = out[:, at] - move(g, at)
-            return carry
-
-        lax.fori_loop(0, groups, again, 0)
-        copies.append(pltpu.make_async_copy(out.at[:, at], out_hbm.at[:, at], sems.at[c]))
-        copies[-1].start()
-
-    rows[...] = inner
+    rows[...] = mine[3]
     lanes = lax.rem(iota((1, LANES), 1), HALF)
     for q in range(plan.owned_pairs):
         every = jnp.zeros((1, LANES), f32)
@@ -499,8 +544,24 @@
         every = every / (1.0 + halves(every, plan.dims))
         centroids[2 * q : 2 * q + 1] = every[:, 0 : plan.dims]
         centroids[2 * q + 1 : 2 * q + 2] = pltpu.roll(every, HALF, 1)[:, 0 : plan.dims]
+    last_copy = pltpu.make_async_copy(centroids, centroids_hbm, done)
+    last_copy.start()
+    copies = []
+    for c in range(plan.chunks):
+        at = plan.at(c)
+        out[:, at] = xs[:, at]
+
+        def again(g, carry):
+            out[:, at] = out[:, at] - move(g, at)
+            return carry
+
+        lax.fori_loop(0, groups, again, 0)
+        copies.append(pltpu.make_async_copy(out.at[:, at], out_hbm.at[:, at], sems.at[c]))
+        copies[-1].start()
+
     for copy in copies:
         copy.wait()
+    last_copy.wait()
 
 
 VMEM = pl.BlockSpec(memory_space=pltpu.VMEM)
@@ -545,13 +606,18 @@
             pltpu.SMEM((4,), i32),
             pltpu.SMEM((plan.local,), f32),
         ),
-        in_specs=[SMEM, SMEM, SMEM, VMEM, WHERE],
+        in_specs=[WHERE] * 5,
         out_specs=(VMEM,) * 7 + (SMEM,) * 2,
         scratch_shapes=[
-            pltpu.SMEM((plan.batches,), i32),
+            pltpu.SMEM(pop.shape, i32),
+            pltpu.SMEM(lam.shape, f32),
+            pltpu.SMEM(scale.shape, f32),
+            pltpu.VMEM(means.shape, f32),
+            pltpu.SMEM((plan.batches + 1,), i32),
             pltpu.VMEM((k, LANES), f32),
             pltpu.VMEM((8, cells), f32),
             pltpu.SemaphoreType.DMA((plan.chunks,)),
+            pltpu.SemaphoreType.DMA((4,)),
         ],
     )(pop, lam, scale, means, x)
     prior, counts, sizes, places, parts, xs = map(hold, (prior, counts, sizes, places, parts, xs))
@@ -562,7 +628,7 @@
         name="moment",
         compiler_params=params,
         out_shape=(
-            kept((plan.devices, 3 * plan.pairs, LANES)),
+            kept((plan.devices * 3 * plan.part, LANES)),
             kept((k, cells), bf16),
             kept((k, cells), bf16),
             kept((plan.groups * plan.depth, LANES)),
@@ -576,8 +642,22 @@
         ],
     )(info, ridges, ids, prior, counts, sizes, places, parts)
     a1, a2, moments = map(hold, (a1, a2, moments))
-    got = hold(lax.all_to_all(send, AXES, 0, 0, tiled=True))
-    marks = 6 + plan.reach * (4 if plan.lone else 2)
+    rows = send.shape[0]
+    got = lax.all_to_all(send.reshape(rows, 1, LANES), AXES, 0, 0, tiled=True)
+    got = hold(got.reshape(rows, LANES))
+    marks = plan.fixed_marks + plan.reach * (4 if plan.lone else 2)
+    mine, theirs = pl.pallas_call(
+        bound(reduce_kernel, plan, "reduce"),
+        name="reduce",
+        compiler_params=params,
+        out_shape=(kept((4, plan.pairs, LANES)), kept((3 * plan.part, LANES))),
+        in_specs=[SMEM] + [VMEM] * 2,
+        out_specs=(VMEM,) * 2,
+        scratch_shapes=[pltpu.VMEM((marks, plan.devices, LANES), f32)],
+    )(info, got, ids)
+    mine = hold(mine)
+    swap = [(i, i + 1 - 2 * (i % 2)) for i in range(plan.devices)]
+    theirs = hold(lax.ppermute(theirs, AXES, swap))
     corrected, centroids = pl.pallas_call(
         bound(correct_kernel, plan, "correct"),
         name="correct",
@@ -587,16 +667,17 @@
             jax.ShapeDtypeStruct((k // plan.rows, plan.dims), f32),
         ),
         in_specs=[SMEM] * 2 + [VMEM] * 7,
-        out_specs=(WHERE, VMEM),
+        out_specs=(WHERE, WHERE),
         scratch_shapes=[
-            pltpu.VMEM((marks, plan.devices, LANES), f32),
             pltpu.VMEM((plan.groups, LANES, plan.depth), bf16),
             pltpu.VMEM((plan.pairs, LANES), f32),
             pltpu.VMEM((k, LANES), f32),
             pltpu.VMEM((plan.dims, cells), f32),
+            pltpu.VMEM((k // plan.rows, plan.dims), f32),
             pltpu.SemaphoreType.DMA((plan.chunks,)),
+            pltpu.SemaphoreType.DMA,
         ],
-    )(info, ridges, got, ids, a1, a2, moments, places, xs)
+    )(info, ridges, mine, theirs, a1, a2, moments, places, xs)
     return corrected, centroids
 
 

time: 38.7 us -> 36 us (0.930); the launches traced: 39.5 us -> 35.9 us
  blocking collectives: 29.3 us -> 25 us
  waiting for transfers between devices: 0 us -> 0.83 us
  Pallas kernels: 9.58 us -> 8.94 us
  starting transfers between devices: 0 us -> 0.51 us
    all_to_all x1, blocking collectives: 15 us -> 10.7 us  [body(): got = lax.all_to_all(send.reshape(rows, 1, LANES), AXES, 0, 0, tiled=True)]
    ppermute x0 -> x1, waiting for transfers between devices: none -> 0.83 us  [body(): theirs = hold(lax.ppermute(theirs, AXES, swap))]
    pallas_call x1, Pallas kernels: 4.11 us -> 3.4 us  [body(): pl.pallas_call(bound(correct_kernel, plan, 'correct'), name='correct', co...]
    ppermute x0 -> x1, starting transfers between devices: none -> 0.51 us  [body(): theirs = hold(lax.ppermute(theirs, AXES, swap))]
  transfers between devices with their start and end apart: 0 -> 1, of which waited for: 0 -> 1; matrix products, arithmetic and copies ran while one was open for 0% -> 0% of each run, Pallas kernels for 0% -> 0%
where the time goes in v3:
time: 36 us; the launch traced here: 35.9 us
  blocking collectives  25 us (69%)
  Pallas kernels  8.94 us (25%)
  waiting for transfers between devices  0.83 us (2%)
  between operations  0.65 us (2%)
  starting transfers between devices  0.51 us (1%)
    all_to_all x1, blocking collectives, body(): ids = hold(lax.all_to_all(send, AXES, 0, 0, tiled=True))  14.3 us
    all_to_all x1, blocking collectives, body(): got = lax.all_to_all(send.reshape(rows, 1, LANES), AXES, 0, 0, tiled=True)  10.7 us
    pallas_call x1, Pallas kernels, body(): pl.pallas_call(bound(correct_kernel, plan, 'correct'), name='correct', co...  3.4 us
    pallas_call x1, Pallas kernels, body(): pl.pallas_call(bound(count_kernel, plan, 'count'), name='count', out_shap...  2.86 us
    pallas_call x1, Pallas kernels, body(): pl.pallas_call(bound(moment_kernel, plan, 'moment'), name='moment', compi...  2.34 us
    ppermute x1, waiting for transfers between devices, body(): theirs = hold(lax.ppermute(theirs, AXES, swap))  0.83 us
  transfers between devices with their start and end apart: 1, of which 1 were waited for; matrix products, arithmetic and copies ran while one was open for 0% of the time, Pallas kernels for 0%

profile of v3, /device:TPU:0, one launch (start us, length us, event | category | flops | bytes accessed | tf_op | source)
XLA Modules:
  0.0 35.9 jit_solution(7555726347309037430)
XLA Ops:
  0.6 2.9 %count.1 = (f32[32,128]{1,0:T(8,128)S(1)}, f32[16,4096]{1,0:T(8,128)S(1)}, f32[7,16,128]{2,1,0:T(8,128)S(1)}, f32[7,128]{1,0:T(8,128)S(1)}, bf16[16,4096]{1,0:T(...) custom-call(s32[200]{0:T(256)} %refs_0_.1, ...), custom_call_target="tpu_custom_call" | custom-call | tf_op jit(solution)/shard_map/count/pallas_call | solution.py:595
  3.5 14.3 %all_to_all.16 = f32[32,1,128]{2,1,0:T(1,128)S(1)} all-to-all(f32[32,1,128]{2,1,0:T(1,128)S(1)} %bitcast.12), channel_id=1, replica_groups=mesh['cells'=8,'grp'=4] {'cells','grp'}, dimensions={0} | all-to-all | bytes 32768 | tf_op jit(solution)/shard_map/all_to_all | solution.py:625
  17.8 2.3 %moment.1 = (f32[384,128]{1,0:T(8,128)S(1)}, bf16[16,4096]{1,0:T(8,128)(2,1)S(1)}, bf16[16,4096]{1,0:T(8,128)(2,1)S(1)}, f32[1792,128]{1,0:T(8,128)S(1)}) custom-call(s32[4]{0:T(128)S(4)} %get-tuple-element.17.refs_0_, f32[112]{0:T(128)S(4)} %get-tuple-element.18.refs_1_, f32[32,128]{1,0:T(8,128)S(1)} %bitcast.10, f32[16,4096]{1,0:T(8,128)S(1)} %get-tuple-element.20.refs_3_, ...), custom_call_target="tpu_custom_call" | custom-call | tf_op jit(solution)/shard_map/moment/pallas_call | solution.py:626
  20.2 10.7 %all_to_all.17 = f32[384,1,128]{2,1,0:T(1,128)S(1)} all-to-all(f32[384,1,128]{2,1,0:T(1,128)S(1)} %bitcast.9), channel_id=1, replica_groups=mesh['cells'=8,'grp'=4] {'cells','grp'}, dimensions={0} | all-to-all | bytes 393216 | tf_op jit(solution)/shard_map/all_to_all | solution.py:646
  30.8 0.3 reduce.1
  31.2 0.5 %collective-permute-start = (f32[12,128]{1,0:T(8,128)S(1)}, f32[12,128]{1,0:T(8,128)S(1)}, u32[]{:S(2)}, u32[]{:S(2)}) collective-permute-start(f32[12,128]{1,0:T(8,128)S(1)} %get-tuple-element.27), channel_id=1, source_target_pairs={{0,1},{1,0},{2,3},{3,2},{4,5},{5,4},{6,7},{7,6},{8,9},{9,8},{10,11... | collective-permute-start | bytes 18440 | tf_op jit(solution)/shard_map/ppermute | solution.py:660
  31.7 0.8 %collective-permute-done.refs_3_ = f32[12,128]{1,0:T(8,128)S(1)} collective-permute-done((f32[12,128]{1,0:T(8,128)S(1)}, f32[12,128]{1,0:T(8,128)S(1)}, u32[]{:S(2)}, u32[]{:S(2)}) %collective-permute-start) | collective-permute-done | bytes 6176 | tf_op jit(solution)/shard_map/ppermute | solution.py:660
  32.5 3.4 %correct.1 = (f32[50,4096]{1,0:T(8,128)}, f32[2,50]{1,0:T(2,128)}) custom-call(s32[4]{0:T(128)S(4)} %get-tuple-element.17.refs_0_, f32[112]{0:T(128)S(4)} %get-tuple-element.18.refs_1_, f32[4,8,128]{2,1,0:T(8,128)S(1)} %get-tuple-element.26.refs_2_, f32[12,128]{1,0:T(8,128)S(1)} %collective-permute-done.refs_3_, ...), custom_call_target="tpu_custom_call" | custom-call | tf_op jit(solution)/shard_map/correct/pallas_call | solution.py:661
Async XLA Ops:
  31.2 1.3 %collective-permute-start = (f32[12,128]{1,0:T(8,128)S(1)}, f32[12,128]{1,0:T(8,128)S(1)}, u32[]{:S(2)}, u32[]{:S(2)}) collective-permute-start(f32[12,128]{1,0:T(8,128)S(1)} %get-tuple-element.27), channel_id=1, source_target_pairs={{0,1},{1,0},{2,3},{3,2},{4,5},{5,4},{6,7},{7,6},{8,9},{9,8},{10,11... | collective-permute-start | bytes 18440 | tf_op jit(solution)/shard_map/ppermute | solution.py:660

commit v4 on v3

--- a/solution.py
+++ b/solution.py
@@ -95,6 +95,9 @@
         self.owned_pairs = self.clusters // self.rows // 2
         self.keep = self.devices * self.pairs * 3 * LANES * 4 <= 1 << 20
         self.fixed_marks = 10
+        self.window = min(self.group, 4)
+        self.piece = min(self.cells, 512)
+        self.pieces = self.cells // self.piece
         self.chunk = min(self.cells, 1024)
         self.chunks = self.cells // self.chunk
 
@@ -120,9 +123,8 @@
     for copy in inputs + copies:
         copy.start()
     offset = (lax.axis_index("cells") * plan.cols + lax.axis_index("grp")) * plan.cells
-    for copy in inputs:
+    for copy in inputs + copies:
         copy.wait()
-    copies[0].wait()
     running, first = jnp.int32(0), jnp.int32(0)
     for b in range(plan.batches):
         running = running + pop[b]
@@ -160,8 +162,6 @@
     rest = [jnp.zeros(shape, f32)] * ((HALF - low) // 8 - 1)
     for c in range(plan.chunks):
         at = plan.at(c)
-        if c:
-            copies[c].wait()
         if over:
             moved = pltpu.roll(xs[plan.dims - 8 : plan.dims, at], over, 0)
             tail = jnp.where(tail_row < over, moved, constant)
@@ -179,12 +179,15 @@
         chance = raised / jnp.sum(raised, axis=0, keepdims=True)
         prior[:, at] = chance
 
-    def following(held):
-        return held[0] + 1, ends[held[0] + 1]
-
-    last, unused = lax.while_loop(
-        lambda held: held[1] < offset + plan.cells, following, (first, ends[first])
-    )
+    last = first
+    for c in range(plan.pieces + 1):
+        bound = offset + min(c * plan.piece, plan.cells - 1)
+
+        def beyond(b, bound=bound):
+            return ends[b] <= bound
+
+        last = lax.while_loop(beyond, lambda b: b + 1, last)
+        info[4 + c] = last - first
     segments = last - first + 1
     tiles = lax.div(segments + TILE - 1, TILE)
     info[0], info[1], info[2] = first, last, segments
@@ -255,18 +258,30 @@
     send[...] = jnp.broadcast_to(out, send.shape)
 
 
-def masked(plan, a1, a2, places, g, at):
-    k = plan.clusters
-    width = at.stop - at.start
-    shape = (TILE, width)
-    base = jnp.full(shape, (g * plan.group).astype(f32) if not isinstance(g, int) else f32(g * plan.group))
-    relative = places[:, at] - base.astype(bf16)
-    out = []
-    for a in (a1[:, at], a2[:, at]):
-        for j in range(plan.group):
-            inside = jnp.concatenate([relative] * (k // TILE), axis=0) == bf16(j)
-            out.append(jnp.where(inside, a, bf16(0)))
-    return jnp.concatenate(out, axis=0)
+def masked(plan, a1, a2, places, base, at, order):
+    base = jnp.full((TILE, plan.piece), base.astype(f32)).astype(bf16)
+    relative = jnp.concatenate([places[:, at] - base] * (plan.clusters // TILE), axis=0)
+    inside = [relative == bf16(j) for j in range(plan.window)]
+    parts = [
+        jnp.concatenate([jnp.where(here, a[:, at], bf16(0)) for here in inside], axis=0) for a in (a1, a2)
+    ]
+    return jnp.concatenate([parts[i] for i in order], axis=0)
+
+
+def windows(plan, info, step):
+    for c in range(plan.pieces):
+        step(c, info[4 + c])
+    more = [lax.div(info[5 + c] - info[4 + c], plan.window) for c in range(plan.pieces)]
+
+    @pl.when(sum(more) > 0)
+    def rest():
+        for c in range(plan.pieces):
+
+            def again(w, carry, c=c):
+                step(c, info[4 + c] + w * plan.window)
+                return carry
+
+            lax.fori_loop(1, more[c] + 1, again, 0)
 
 
 def moment_kernel(
@@ -326,16 +341,30 @@
 
     sums[...] = jnp.zeros_like(sums)
 
+    def clear(g, carry):
+        moments[pl.ds(pl.multiple_of(g * plan.depth, plan.depth), plan.depth), :] = jnp.zeros(
+            (plan.depth, LANES), f32
+        )
+        return carry
+
+    lax.fori_loop(0, groups + 1, clear, 0)
+    size = plan.window * k
+
+    def collect(c, base):
+        at = slice(c * plan.piece, (c + 1) * plan.piece)
+        both = lax.dot_general(
+            masked(plan, a1, a2, places, base, at, (0, 1)), parts[:, at], BY_CELLS, preferred_element_type=f32
+        )
+        to = pl.ds(pl.multiple_of(base * k, k), size)
+        moments[to, :] = moments[to, :] + (both[0:size] + both[size:])
+
+    windows(plan, info, collect)
+
     def gather(g, carry):
-        both = jnp.zeros((2 * plan.depth, LANES), f32)
-        for c in range(plan.chunks):
-            at = plan.at(c)
-            both = both + lax.dot_general(
-                masked(plan, a1, a2, places, g, at), parts[:, at], BY_CELLS, preferred_element_type=f32
-            )
-        both = both[0 : plan.depth] + both[plan.depth :]
+        to = pl.ds(pl.multiple_of(g * plan.depth, plan.depth), plan.depth)
+        both = moments[to, :]
         both = both + pltpu.roll(both, HALF, 1)
-        moments[pl.ds(pl.multiple_of(g * plan.depth, plan.depth), plan.depth), :] = both
+        moments[to, :] = both
         mass = lane_of(both, plan.dims)
         inner, head, tail, every = sums[0], sums[1], sums[2], sums[3]
         for j in range(plan.group):
@@ -502,8 +531,6 @@
         return unpack_pairs(spread, jnp.where(low != odd, mine[i], piece))
 
     intercept, first_sum, last_sum = both(0), both(1), both(2)
-    left = iota((k, LANES), 1) < HALF
-
     def slope(g, carry):
         start = pl.multiple_of(g * plan.depth, plan.depth)
         held = moments[pl.ds(start, plan.depth), :]
@@ -515,21 +542,16 @@
             part = jnp.where(s == segments - 1, last_sum, part)
             mass = lane_of(part, plan.dims)
             ridge = ridges[s]
-            s1, s2 = split((part - mass * intercept) / (mass + ridge), 2)
-            made.append(jnp.where(left, s1.astype(f32), s2.astype(f32)))
-        slopes[g] = jnp.transpose(jnp.concatenate(made, axis=0)).astype(bf16)
+            made.append((part - mass * intercept) / (mass + ridge))
+        for i, piece in enumerate(split(jnp.concatenate(made, axis=0), 2)):
+            slopes[i, pl.ds(start, plan.depth), :] = piece
         return carry
 
     lax.fori_loop(0, groups, slope, 0)
-
-    def move(g, at):
-        mine = slopes[g]
-        moved = jnp.dot(
-            jnp.concatenate([mine, mine], axis=1),
-            masked(plan, a1, a2, places, g, at),
-            preferred_element_type=f32,
-        )
-        return (moved[0:HALF] + moved[HALF:])[0 : plan.dims]
+    blank = jnp.zeros((plan.depth, LANES), bf16)
+    for i in range(2):
+        slopes[i, pl.ds(pl.multiple_of(groups * plan.depth, plan.depth), plan.depth), :] = blank
+    size = plan.window * k
 
     rows[...] = mine[3]
     lanes = lax.rem(iota((1, LANES), 1), HALF)
@@ -546,19 +568,26 @@
         centroids[2 * q + 1 : 2 * q + 2] = pltpu.roll(every, HALF, 1)[:, 0 : plan.dims]
     last_copy = pltpu.make_async_copy(centroids, centroids_hbm, done)
     last_copy.start()
+    out[...] = xs[...]
+
+    def move(c, base):
+        at = slice(c * plan.piece, (c + 1) * plan.piece)
+        rows_of = pl.ds(pl.multiple_of(base * k, k), size)
+        large, fine = slopes[0, rows_of, 0:HALF], slopes[1, rows_of, 0:HALF]
+        moved = lax.dot_general(
+            jnp.concatenate([large, fine, large], axis=0),
+            masked(plan, a1, a2, places, base, at, (0, 0, 1)),
+            BY_ROWS,
+            preferred_element_type=f32,
+        )
+        out[:, at] = out[:, at] - moved[0 : plan.dims]
+
+    windows(plan, info, move)
     copies = []
     for c in range(plan.chunks):
         at = plan.at(c)
-        out[:, at] = xs[:, at]
-
-        def again(g, carry):
-            out[:, at] = out[:, at] - move(g, at)
-            return carry
-
-        lax.fori_loop(0, groups, again, 0)
         copies.append(pltpu.make_async_copy(out.at[:, at], out_hbm.at[:, at], sems.at[c]))
         copies[-1].start()
-
     for copy in copies:
         copy.wait()
     last_copy.wait()
@@ -603,7 +632,7 @@
             kept((TILE, cells), bf16),
             kept((2 * HALF, cells), bf16),
             kept((plan.dims, cells)),
-            pltpu.SMEM((4,), i32),
+            pltpu.SMEM((5 + plan.pieces,), i32),
             pltpu.SMEM((plan.local,), f32),
         ),
         in_specs=[WHERE] * 5,
@@ -631,7 +660,7 @@
             kept((plan.devices * 3 * plan.part, LANES)),
             kept((k, cells), bf16),
             kept((k, cells), bf16),
-            kept((plan.groups * plan.depth, LANES)),
+            kept(((plan.groups + 1) * plan.depth, LANES)),
         ),
         in_specs=[SMEM] * 2 + [VMEM] * 6,
         out_specs=(VMEM,) * 4,
@@ -669,7 +698,7 @@
         in_specs=[SMEM] * 2 + [VMEM] * 7,
         out_specs=(WHERE, WHERE),
         scratch_shapes=[
-            pltpu.VMEM((plan.groups, LANES, plan.depth), bf16),
+            pltpu.VMEM((2, (plan.groups + 1) * plan.depth, LANES), bf16),
             pltpu.VMEM((plan.pairs, LANES), f32),
             pltpu.VMEM((k, LANES), f32),
             pltpu.VMEM((plan.dims, cells), f32),

time: 36 us -> 33 us (0.917)
  Pallas kernels: 8.94 us -> 5.87 us
    pallas_call x1, Pallas kernels: 3.4 us -> 1.61 us  [body(): pl.pallas_call(bound(correct_kernel, plan, 'correct'), name='correct', co...]
    pallas_call x1, Pallas kernels: 2.34 us -> 1.25 us  [body(): pl.pallas_call(bound(moment_kernel, plan, 'moment'), name='moment', compi...]
where the time goes in v4:
time: 33 us; the launch traced here: 32.8 us
  blocking collectives  25 us (76%)
  Pallas kernels  5.87 us (18%)
  waiting for transfers between devices  0.83 us (3%)
  between operations  0.65 us (2%)
  starting transfers between devices  0.51 us (2%)
    all_to_all x1, blocking collectives, body(): ids = hold(lax.all_to_all(send, AXES, 0, 0, tiled=True))  14.3 us
    all_to_all x1, blocking collectives, body(): got = lax.all_to_all(send.reshape(rows, 1, LANES), AXES, 0, 0, tiled=True)  10.7 us
    pallas_call x1, Pallas kernels, body(): pl.pallas_call(bound(count_kernel, plan, 'count'), name='count', out_shap...  2.68 us
    pallas_call x1, Pallas kernels, body(): pl.pallas_call(bound(correct_kernel, plan, 'correct'), name='correct', co...  1.61 us
    pallas_call x1, Pallas kernels, body(): pl.pallas_call(bound(moment_kernel, plan, 'moment'), name='moment', compi...  1.25 us
    ppermute x1, waiting for transfers between devices, body(): theirs = hold(lax.ppermute(theirs, AXES, swap))  0.83 us
  transfers between devices with their start and end apart: 1, of which 1 were waited for; matrix products, arithmetic and copies ran while one was open for 0% of the time, Pallas kernels for 0%

profile of v4, /device:TPU:0, one launch (start us, length us, event | category | flops | bytes accessed | tf_op | source)
XLA Modules:
  0.0 32.8 jit_solution(5651795767325948101)
XLA Ops:
  0.6 2.7 %count.1 = (f32[32,128]{1,0:T(8,128)S(1)}, f32[16,4096]{1,0:T(8,128)S(1)}, f32[7,16,128]{2,1,0:T(8,128)S(1)}, f32[7,128]{1,0:T(8,128)S(1)}, bf16[16,4096]{1,0:T(...) custom-call(s32[200]{0:T(256)} %refs_0_.1, ...), custom_call_target="tpu_custom_call" | custom-call | tf_op jit(solution)/shard_map/count/pallas_call | solution.py:624
  3.3 14.3 %all_to_all.16 = f32[32,1,128]{2,1,0:T(1,128)S(1)} all-to-all(f32[32,1,128]{2,1,0:T(1,128)S(1)} %bitcast.12), channel_id=1, replica_groups=mesh['cells'=8,'grp'=4] {'cells','grp'}, dimensions={0} | all-to-all | bytes 32768 | tf_op jit(solution)/shard_map/all_to_all | solution.py:654
  17.6 1.2 %moment.1 = (f32[384,128]{1,0:T(8,128)S(1)}, bf16[16,4096]{1,0:T(8,128)(2,1)S(1)}, bf16[16,4096]{1,0:T(8,128)(2,1)S(1)}, f32[1920,128]{1,0:T(8,128)S(1)}) custom-call(s32[13]{0:T(128)S(4)} %get-tuple-element.17.refs_0_, f32[112]{0:T(128)S(4)} %get-tuple-element.18.refs_1_, f32[32,128]{1,0:T(8,128)S(1)} %bitcast.10, ...), custom_call_target="tpu_custom_call" | custom-call | tf_op jit(solution)/shard_map/moment/pallas_call | solution.py:655
  18.9 10.7 %all_to_all.17 = f32[384,1,128]{2,1,0:T(1,128)S(1)} all-to-all(f32[384,1,128]{2,1,0:T(1,128)S(1)} %bitcast.9), channel_id=1, replica_groups=mesh['cells'=8,'grp'=4] {'cells','grp'}, dimensions={0} | all-to-all | bytes 393216 | tf_op jit(solution)/shard_map/all_to_all | solution.py:675
  29.5 0.3 %reduce.1 = (f32[4,8,128]{2,1,0:T(8,128)S(1)}, f32[12,128]{1,0:T(8,128)S(1)}) custom-call(s32[13]{0:T(128)S(4)} %get-tuple-element.17.refs_0_, f32[384,128]{1,0:T(8,128)S(1)} %bitcast.8, f32[32,128]{1,0:T(8,128)S(1)} %bitcast.11), custom_call_target="tpu_custom_call" | custom-call | tf_op jit(solution)/shard_map/reduce/pallas_call | solution.py:678
  29.9 0.5 %collective-permute-start = (f32[12,128]{1,0:T(8,128)S(1)}, f32[12,128]{1,0:T(8,128)S(1)}, u32[]{:S(2)}, u32[]{:S(2)}) collective-permute-start(f32[12,128]{1,0:T(8,128)S(1)} %get-tuple-element.27), channel_id=1, source_target_pairs={{0,1},{1,0},{2,3},{3,2},{4,5},{5,4},{6,7},{7,6},{8,9},{9,8},{10,11... | collective-permute-start | bytes 18440 | tf_op jit(solution)/shard_map/ppermute | solution.py:689
  30.4 0.8 %collective-permute-done.refs_3_ = f32[12,128]{1,0:T(8,128)S(1)} collective-permute-done((f32[12,128]{1,0:T(8,128)S(1)}, f32[12,128]{1,0:T(8,128)S(1)}, u32[]{:S(2)}, u32[]{:S(2)}) %collective-permute-start) | collective-permute-done | bytes 6176 | tf_op jit(solution)/shard_map/ppermute | solution.py:689
  31.2 1.6 %correct.1 = (f32[50,4096]{1,0:T(8,128)}, f32[2,50]{1,0:T(2,128)}) custom-call(s32[13]{0:T(128)S(4)} %get-tuple-element.17.refs_0_, f32[112]{0:T(128)S(4)} %get-tuple-element.18.refs_1_, f32[4,8,128]{2,1,0:T(8,128)S(1)} %get-tuple-element.26.refs_2_, f32[12,128]{1,0:T(8,128)S(1)} %collective-permute-done.refs_3_, ...), custom_call_target="tpu_custom_call" | custom-call | tf_op jit(solution)/shard_map/correct/pallas_call | solution.py:690
Async XLA Ops:
  29.9 1.3 %collective-permute-start = (f32[12,128]{1,0:T(8,128)S(1)}, f32[12,128]{1,0:T(8,128)S(1)}, u32[]{:S(2)}, u32[]{:S(2)}) collective-permute-start(f32[12,128]{1,0:T(8,128)S(1)} %get-tuple-element.27), channel_id=1, source_target_pairs={{0,1},{1,0},{2,3},{3,2},{4,5},{5,4},{6,7},{7,6},{8,9},{9,8},{10,11... | collective-permute-start | bytes 18440 | tf_op jit(solution)/shard_map/ppermute | solution.py:689

commit v5 on v4

--- a/solution.py
+++ b/solution.py
@@ -9,6 +9,7 @@
 bf16 = jnp.bfloat16
 i32 = jnp.int32
 HALF = 64
+PIECE = 1024
 LANES = 128
 TILE = 16
 AXES = ("cells", "grp")
@@ -87,6 +88,7 @@
         self.group = max(1, LANES // self.clusters)
         self.groups = self.local // self.group
         self.depth = self.group * self.clusters
+        self.table = (self.groups + 1) * self.depth
         self.width = -(-(3 * self.clusters + 4) // LANES) * LANES
         self.pairs = self.clusters // 2
         self.part = self.pairs // 2
@@ -98,7 +100,7 @@
         self.window = min(self.group, 4)
         self.piece = min(self.cells, 512)
         self.pieces = self.cells // self.piece
-        self.chunk = min(self.cells, 1024)
+        self.chunk = min(self.cells, PIECE)
         self.chunks = self.cells // self.chunk
 
     def at(self, c):
@@ -123,14 +125,82 @@
     for copy in inputs + copies:
         copy.start()
     offset = (lax.axis_index("cells") * plan.cols + lax.axis_index("grp")) * plan.cells
-    for copy in inputs + copies:
+    inputs[0].wait()
+    running, base, blocks = jnp.int32(0), jnp.int32(0), jnp.int32(0)
+    for low in range(0, plan.batches, 8):
+        held = [pop[b] for b in range(low, min(low + 8, plan.batches))]
+        while len(held) > 1:
+            held = [sum(held[i : i + 2]) for i in range(0, len(held), 2)]
+        running = running + held[0]
+        base = jnp.where(running <= offset, running, base)
+        blocks = blocks + (running <= offset).astype(i32)
+    first, running = blocks * 8, base
+    for j in range(8):
+        running = running + pop[jnp.minimum(blocks * 8 + j, plan.batches - 1)]
+        base = jnp.where(running <= offset, running, base)
+        first = first + (running <= offset).astype(i32)
+
+    end = base + pop[first] - offset
+    ends[0] = end
+    here = jnp.int32(0)
+    for c in range(plan.pieces + 1):
+        place_of = min(c * plan.piece, plan.cells - 1)
+
+        def onward(held):
+            end = held[1] + pop[first + held[0] + 1]
+            ends[held[0] + 1] = end
+            return held[0] + 1, end
+
+        here, end = lax.while_loop(lambda held, at=place_of: held[1] <= at, onward, (here, end))
+        info[4 + c] = here
+    segments = here + 1
+    last = first + here
+    tiles = lax.div(segments + TILE - 1, TILE)
+    info[0], info[1], info[2] = first, last, segments
+
+    lane = iota((1, LANES), 1)
+    cell = iota((8, plan.cells), 1)
+    half = TILE // 2
+
+    def mark(g, held):
+        for j in range(half):
+            s = g * half + j
+            after = jnp.float32(s + 1) if isinstance(s, int) else (s + 1).astype(f32)
+            held = jnp.where(cell >= ends[jnp.minimum(s, here)], after, held)
+        return held
+
+    def place(held):
+        places[...] = jnp.concatenate([held] * (TILE // 8), axis=0).astype(bf16)
+
+    @pl.when(segments <= half)
+    def few():
+        place(mark(0, jnp.zeros(cell.shape, f32)))
+
+    @pl.when(segments > half)
+    def many():
+        seg[...] = mark(0, jnp.zeros(cell.shape, f32))
+
+        def locate(g, carry):
+            seg[...] = mark(g, seg[...])
+            return carry
+
+        lax.fori_loop(1, lax.div(segments + half - 1, half), locate, 0)
+        place(seg[...])
+
+    for copy in inputs[1:]:
         copy.wait()
-    running, first = jnp.int32(0), jnp.int32(0)
-    for b in range(plan.batches):
-        running = running + pop[b]
-        ends[b] = running
-        first = first + (running <= offset).astype(i32)
-
+
+    def note(g, carry):
+        row = jnp.zeros((1, LANES), f32)
+        for j in range(TILE):
+            b = jnp.minimum(first + g * TILE + j, plan.batches - 1)
+            ridges[g * TILE + j] = lam[b]
+            row = jnp.where(lane == j, pop[b].astype(f32), row)
+        sizes[pl.ds(g, 1), :] = row
+        return carry
+
+    lax.fori_loop(1, tiles, note, 0)
+    note(0, 0)
     ms[...] = jnp.zeros_like(ms)
     ms[:, 0 : plan.dims] = means[...]
     m = ms[...]
@@ -160,7 +230,8 @@
     tail_row = iota(shape, 0)
     constant = jnp.where(tail_row == over, 1.0, 0.0)
     rest = [jnp.zeros(shape, f32)] * ((HALF - low) // 8 - 1)
-    for c in range(plan.chunks):
+
+    def affinity(c):
         at = plan.at(c)
         if over:
             moved = pltpu.roll(xs[plan.dims - 8 : plan.dims, at], over, 0)
@@ -174,55 +245,35 @@
         stacked = jnp.concatenate([x1, x2, x3, jnp.zeros_like(x1)], axis=0)
         dots = jnp.dot(weights, stacked, preferred_element_type=f32)
         dots = dots[0:k] + dots[k : 2 * k] + dots[2 * k : 3 * k]
-        scores = (2.0 * dots - lengths) * inverse
+        return (2.0 * dots - lengths) * inverse
+
+    spots = iota((TILE, plan.chunk), 0).astype(f32).astype(bf16)
+
+    def finish(c, scores):
+        at = plan.at(c)
         raised = jnp.exp(scores - jnp.max(scores, axis=0, keepdims=True))
         chance = raised / jnp.sum(raised, axis=0, keepdims=True)
         prior[:, at] = chance
-
-    last = first
-    for c in range(plan.pieces + 1):
-        bound = offset + min(c * plan.piece, plan.cells - 1)
-
-        def beyond(b, bound=bound):
-            return ends[b] <= bound
-
-        last = lax.while_loop(beyond, lambda b: b + 1, last)
-        info[4 + c] = last - first
-    segments = last - first + 1
-    tiles = lax.div(segments + TILE - 1, TILE)
-    info[0], info[1], info[2] = first, last, segments
-
-    lane = iota((1, LANES), 1)
-    cell = iota((8, plan.cells), 1)
-    half = TILE // 2
-    seg[...] = jnp.zeros_like(seg)
-
-    def locate(g, carry):
-        held = seg[...]
-        for j in range(half):
-            s = g * half + j
-            b = jnp.minimum(first + s, plan.batches - 1)
-            held = jnp.where(cell >= ends[b] - offset, (s + 1).astype(f32), held)
-        seg[...] = held
-        return carry
-
-    lax.fori_loop(0, lax.div(segments + half - 1, half), locate, 0)
-    places[...] = jnp.concatenate([seg[...]] * (TILE // 8), axis=0).astype(bf16)
-
-    def note(g, carry):
-        row = jnp.zeros((1, LANES), f32)
-        for j in range(TILE):
-            b = jnp.minimum(first + g * TILE + j, plan.batches - 1)
-            ridges[g * TILE + j] = lam[b]
-            row = jnp.where(lane == j, pop[b].astype(f32), row)
-        sizes[pl.ds(g, 1), :] = row
-        return carry
-
-    lax.fori_loop(0, tiles, note, 0)
+        hot = jnp.where(places[:, at] == spots, bf16(1), bf16(0))
+        return lax.dot_general(
+            jnp.concatenate(split(chance, 3), axis=0), hot, BY_CELLS, preferred_element_type=f32
+        )
+
+    found = jnp.zeros((3 * k, TILE), f32)
+    scores = following = None
+    for c in range(plan.chunks + 1):
+        if c < plan.chunks:
+            copies[c].wait()
+            following = affinity(c)
+        if c:
+            found = found + finish(c - 1, scores)
+        scores = following
 
     def settle(g, found):
         found = found[0:k] + found[k : 2 * k] + found[2 * k :]
         counts[g] = jnp.concatenate([found, jnp.zeros((k, LANES - TILE), f32)], axis=1)
+
+    settle(0, found)
 
     def count(g, carry):
         rows = (iota((TILE, plan.cells), 0) + g * TILE).astype(f32).astype(bf16)
@@ -235,11 +286,10 @@
         )
         return carry
 
-    lax.fori_loop(0, tiles, count, 0)
+    lax.fori_loop(1, tiles, count, 0)
 
     every = lax.fori_loop(1, tiles, lambda g, total: total + counts[g], counts[0])
     total = jnp.sum(every, axis=1, keepdims=True)
-    here = segments - 1
     end = counts[lax.div(here, TILE)]
     wide = iota((k, LANES), 1)
     last_count = jnp.sum(jnp.where(wide == lax.rem(here, TILE), end, 0.0), axis=1, keepdims=True)
@@ -268,20 +318,18 @@
     return jnp.concatenate([parts[i] for i in order], axis=0)
 
 
-def windows(plan, info, step):
+def extra_windows(plan, info):
+    return [lax.div(info[5 + c] - info[4 + c], plan.window) for c in range(plan.pieces)]
+
+
+def other_windows(plan, info, more, step):
     for c in range(plan.pieces):
-        step(c, info[4 + c])
-    more = [lax.div(info[5 + c] - info[4 + c], plan.window) for c in range(plan.pieces)]
-
-    @pl.when(sum(more) > 0)
-    def rest():
-        for c in range(plan.pieces):
-
-            def again(w, carry, c=c):
-                step(c, info[4 + c] + w * plan.window)
-                return carry
-
-            lax.fori_loop(1, more[c] + 1, again, 0)
+
+        def again(w, carry, c=c):
+            step(c, info[4 + c] + w * plan.window)
+            return carry
+
+        lax.fori_loop(1, more[c] + 1, again, 0)
 
 
 def moment_kernel(
@@ -324,31 +372,11 @@
         return jnp.dot(weights, hot, preferred_element_type=f32)
 
     weights = factors(0)
-    for c in range(plan.chunks):
-        wide[:, plan.at(c)] = factor_of(weights, 0, plan.at(c))
-
-    def more(g, carry):
-        weights = factors(g)
-        for c in range(plan.chunks):
-            wide[:, plan.at(c)] += factor_of(weights, g, plan.at(c))
-        return carry
-
-    lax.fori_loop(1, tiles, more, 0)
-    for c in range(plan.chunks):
-        at = plan.at(c)
-        raised = prior[:, at] * wide[:, at]
+    size = plan.window * k
+
+    def settle(at, factor):
+        raised = prior[:, at] * factor
         a1[:, at], a2[:, at] = split(raised / jnp.sum(raised, axis=0, keepdims=True), 2)
-
-    sums[...] = jnp.zeros_like(sums)
-
-    def clear(g, carry):
-        moments[pl.ds(pl.multiple_of(g * plan.depth, plan.depth), plan.depth), :] = jnp.zeros(
-            (plan.depth, LANES), f32
-        )
-        return carry
-
-    lax.fori_loop(0, groups + 1, clear, 0)
-    size = plan.window * k
 
     def collect(c, base):
         at = slice(c * plan.piece, (c + 1) * plan.piece)
@@ -358,7 +386,45 @@
         to = pl.ds(pl.multiple_of(base * k, k), size)
         moments[to, :] = moments[to, :] + (both[0:size] + both[size:])
 
-    windows(plan, info, collect)
+    more = extra_windows(plan, info)
+
+    @pl.when(tiles == 1)
+    def straight():
+        spare = (TILE + plan.window) * k
+        moments[0:spare, :] = jnp.zeros((spare, LANES), f32)
+        for c in range(plan.chunks):
+            settle(plan.at(c), factor_of(weights, 0, plan.at(c)))
+        for c in range(plan.pieces):
+            collect(c, info[4 + c])
+
+    @pl.when(tiles > 1)
+    def general():
+        def clear(g, carry):
+            moments[pl.ds(pl.multiple_of(g * plan.depth, plan.depth), plan.depth), :] = jnp.zeros(
+                (plan.depth, LANES), f32
+            )
+            return carry
+
+        lax.fori_loop(0, groups + 1, clear, 0)
+        wide[...] = jnp.zeros_like(wide)
+
+        def add(g, carry):
+            weights = factors(g)
+            for c in range(plan.chunks):
+                wide[:, plan.at(c)] += factor_of(weights, g, plan.at(c))
+            return carry
+
+        lax.fori_loop(0, tiles, add, 0)
+        for c in range(plan.chunks):
+            settle(plan.at(c), wide[:, plan.at(c)])
+        for c in range(plan.pieces):
+            collect(c, info[4 + c])
+
+    @pl.when(sum(more) > 0)
+    def others():
+        other_windows(plan, info, more, collect)
+
+    sums[...] = jnp.zeros_like(sums)
 
     def gather(g, carry):
         to = pl.ds(pl.multiple_of(g * plan.depth, plan.depth), plan.depth)
@@ -568,26 +634,45 @@
         centroids[2 * q + 1 : 2 * q + 2] = pltpu.roll(every, HALF, 1)[:, 0 : plan.dims]
     last_copy = pltpu.make_async_copy(centroids, centroids_hbm, done)
     last_copy.start()
-    out[...] = xs[...]
-
-    def move(c, base):
+    copies = []
+    for c in range(plan.pieces):
+        at = slice(c * plan.piece, (c + 1) * plan.piece)
+        copies.append(pltpu.make_async_copy(out.at[:, at], out_hbm.at[:, at], sems.at[c]))
+
+    def moved(c, base):
         at = slice(c * plan.piece, (c + 1) * plan.piece)
         rows_of = pl.ds(pl.multiple_of(base * k, k), size)
         large, fine = slopes[0, rows_of, 0:HALF], slopes[1, rows_of, 0:HALF]
-        moved = lax.dot_general(
+        return lax.dot_general(
             jnp.concatenate([large, fine, large], axis=0),
             masked(plan, a1, a2, places, base, at, (0, 0, 1)),
             BY_ROWS,
             preferred_element_type=f32,
-        )
-        out[:, at] = out[:, at] - moved[0 : plan.dims]
-
-    windows(plan, info, move)
-    copies = []
-    for c in range(plan.chunks):
-        at = plan.at(c)
-        copies.append(pltpu.make_async_copy(out.at[:, at], out_hbm.at[:, at], sems.at[c]))
-        copies[-1].start()
+        )[0 : plan.dims]
+
+    more = extra_windows(plan, info)
+
+    @pl.when(sum(more) == 0)
+    def straight():
+        for c in range(plan.pieces):
+            at = slice(c * plan.piece, (c + 1) * plan.piece)
+            out[:, at] = xs[:, at] - moved(c, info[4 + c])
+            copies[c].start()
+
+    @pl.when(sum(more) > 0)
+    def general():
+        for c in range(plan.pieces):
+            at = slice(c * plan.piece, (c + 1) * plan.piece)
+            out[:, at] = xs[:, at] - moved(c, info[4 + c])
+
+        def step(c, base):
+            at = slice(c * plan.piece, (c + 1) * plan.piece)
+            out[:, at] = out[:, at] - moved(c, base)
+
+        other_windows(plan, info, more, step)
+        for copy in copies:
+            copy.start()
+
     for copy in copies:
         copy.wait()
     last_copy.wait()
@@ -642,7 +727,7 @@
             pltpu.SMEM(lam.shape, f32),
             pltpu.SMEM(scale.shape, f32),
             pltpu.VMEM(means.shape, f32),
-            pltpu.SMEM((plan.batches + 1,), i32),
+            pltpu.SMEM((plan.batches,), i32),
             pltpu.VMEM((k, LANES), f32),
             pltpu.VMEM((8, cells), f32),
             pltpu.SemaphoreType.DMA((plan.chunks,)),
@@ -660,7 +745,7 @@
             kept((plan.devices * 3 * plan.part, LANES)),
             kept((k, cells), bf16),
             kept((k, cells), bf16),
-            kept(((plan.groups + 1) * plan.depth, LANES)),
+            kept((plan.table, LANES)),
         ),
         in_specs=[SMEM] * 2 + [VMEM] * 6,
         out_specs=(VMEM,) * 4,
@@ -698,12 +783,12 @@
         in_specs=[SMEM] * 2 + [VMEM] * 7,
         out_specs=(WHERE, WHERE),
         scratch_shapes=[
-            pltpu.VMEM((2, (plan.groups + 1) * plan.depth, LANES), bf16),
+            pltpu.VMEM((2, plan.table, LANES), bf16),
             pltpu.VMEM((plan.pairs, LANES), f32),
             pltpu.VMEM((k, LANES), f32),
             pltpu.VMEM((plan.dims, cells), f32),
             pltpu.VMEM((k // plan.rows, plan.dims), f32),
-            pltpu.SemaphoreType.DMA((plan.chunks,)),
+            pltpu.SemaphoreType.DMA((plan.pieces,)),
             pltpu.SemaphoreType.DMA,
         ],
     )(info, ridges, mine, theirs, a1, a2, moments, places, xs)

time: 33 us -> 32.7 us (level)
  no operation moved by 1% of the time
where the time goes in v5:
time: 32.7 us; the launch traced here: 32.5 us
  blocking collectives  25 us (76%)
  Pallas kernels  5.57 us (17%)
  waiting for transfers between devices  0.83 us (3%)
  between operations  0.65 us (2%)
  starting transfers between devices  0.51 us (2%)
    all_to_all x1, blocking collectives, body(): ids = hold(lax.all_to_all(send, AXES, 0, 0, tiled=True))  14.3 us
    all_to_all x1, blocking collectives, body(): got = lax.all_to_all(send.reshape(rows, 1, LANES), AXES, 0, 0, tiled=True)  10.7 us
    pallas_call x1, Pallas kernels, body(): pl.pallas_call(bound(count_kernel, plan, 'count'), name='count', out_shap...  2.48 us
    pallas_call x1, Pallas kernels, body(): pl.pallas_call(bound(correct_kernel, plan, 'correct'), name='correct', co...  1.62 us
    pallas_call x1, Pallas kernels, body(): pl.pallas_call(bound(moment_kernel, plan, 'moment'), name='moment', compi...  1.14 us
    ppermute x1, waiting for transfers between devices, body(): theirs = hold(lax.ppermute(theirs, AXES, swap))  0.83 us
  transfers between devices with their start and end apart: 1, of which 1 were waited for; matrix products, arithmetic and copies ran while one was open for 0% of the time, Pallas kernels for 0%

profile of v5, /device:TPU:0, one launch (start us, length us, event | category | flops | bytes accessed | tf_op | source)
XLA Modules:
  0.0 32.5 jit_solution(17724320391175443883)
XLA Ops:
  0.6 2.5 %count.1 = (f32[32,128]{1,0:T(8,128)S(1)}, f32[16,4096]{1,0:T(8,128)S(1)}, f32[7,16,128]{2,1,0:T(8,128)S(1)}, f32[7,128]{1,0:T(8,128)S(1)}, bf16[16,4096]{1,0:T(...) custom-call(s32[200]{0:T(256)} %refs_0_.1, ...), custom_call_target="tpu_custom_call" | custom-call | tf_op jit(solution)/shard_map/count/pallas_call | solution.py:709
  3.1 14.3 %all_to_all.16 = f32[32,1,128]{2,1,0:T(1,128)S(1)} all-to-all(f32[32,1,128]{2,1,0:T(1,128)S(1)} %bitcast.12), channel_id=1, replica_groups=mesh['cells'=8,'grp'=4] {'cells','grp'}, dimensions={0} | all-to-all | bytes 32768 | tf_op jit(solution)/shard_map/all_to_all | solution.py:739
  17.4 1.1 %moment.1 = (f32[384,128]{1,0:T(8,128)S(1)}, bf16[16,4096]{1,0:T(8,128)(2,1)S(1)}, bf16[16,4096]{1,0:T(8,128)(2,1)S(1)}, f32[1920,128]{1,0:T(8,128)S(1)}) custom-call(s32[13]{0:T(128)S(4)} %get-tuple-element.17.refs_0_, f32[112]{0:T(128)S(4)} %get-tuple-element.18.refs_1_, f32[32,128]{1,0:T(8,128)S(1)} %bitcast.10, ...), custom_call_target="tpu_custom_call" | custom-call | tf_op jit(solution)/shard_map/moment/pallas_call | solution.py:740
  18.6 10.7 %all_to_all.17 = f32[384,1,128]{2,1,0:T(1,128)S(1)} all-to-all(f32[384,1,128]{2,1,0:T(1,128)S(1)} %bitcast.9), channel_id=1, replica_groups=mesh['cells'=8,'grp'=4] {'cells','grp'}, dimensions={0} | all-to-all | bytes 393216 | tf_op jit(solution)/shard_map/all_to_all | solution.py:760
  29.2 0.3 %reduce.1 = (f32[4,8,128]{2,1,0:T(8,128)S(1)}, f32[12,128]{1,0:T(8,128)S(1)}) custom-call(s32[13]{0:T(128)S(4)} %get-tuple-element.17.refs_0_, f32[384,128]{1,0:T(8,128)S(1)} %bitcast.8, f32[32,128]{1,0:T(8,128)S(1)} %bitcast.11), custom_call_target="tpu_custom_call" | custom-call | tf_op jit(solution)/shard_map/reduce/pallas_call | solution.py:763
  29.6 0.5 %collective-permute-start = (f32[12,128]{1,0:T(8,128)S(1)}, f32[12,128]{1,0:T(8,128)S(1)}, u32[]{:S(2)}, u32[]{:S(2)}) collective-permute-start(f32[12,128]{1,0:T(8,128)S(1)} %get-tuple-element.27), channel_id=1, source_target_pairs={{0,1},{1,0},{2,3},{3,2},{4,5},{5,4},{6,7},{7,6},{8,9},{9,8},{10,11... | collective-permute-start | bytes 18440 | tf_op jit(solution)/shard_map/ppermute | solution.py:774
  30.1 0.8 %collective-permute-done.refs_3_ = f32[12,128]{1,0:T(8,128)S(1)} collective-permute-done((f32[12,128]{1,0:T(8,128)S(1)}, f32[12,128]{1,0:T(8,128)S(1)}, u32[]{:S(2)}, u32[]{:S(2)}) %collective-permute-start) | collective-permute-done | bytes 6176 | tf_op jit(solution)/shard_map/ppermute | solution.py:774
  30.9 1.6 %correct.1 = (f32[50,4096]{1,0:T(8,128)}, f32[2,50]{1,0:T(2,128)}) custom-call(s32[13]{0:T(128)S(4)} %get-tuple-element.17.refs_0_, f32[112]{0:T(128)S(4)} %get-tuple-element.18.refs_1_, f32[4,8,128]{2,1,0:T(8,128)S(1)} %get-tuple-element.26.refs_2_, f32[12,128]{1,0:T(8,128)S(1)} %collective-permute-done.refs_3_, ...), custom_call_target="tpu_custom_call" | custom-call | tf_op jit(solution)/shard_map/correct/pallas_call | solution.py:775
Async XLA Ops:
  29.6 1.3 %collective-permute-start = (f32[12,128]{1,0:T(8,128)S(1)}, f32[12,128]{1,0:T(8,128)S(1)}, u32[]{:S(2)}, u32[]{:S(2)}) collective-permute-start(f32[12,128]{1,0:T(8,128)S(1)} %get-tuple-element.27), channel_id=1, source_target_pairs={{0,1},{1,0},{2,3},{3,2},{4,5},{5,4},{6,7},{7,6},{8,9},{9,8},{10,11... | collective-permute-start | bytes 18440 | tf_op jit(solution)/shard_map/ppermute | solution.py:774

commit v6 on v5

--- a/solution.py
+++ b/solution.py
@@ -9,7 +9,7 @@
 bf16 = jnp.bfloat16
 i32 = jnp.int32
 HALF = 64
-PIECE = 1024
+PIECE = 4096
 LANES = 128
 TILE = 16
 AXES = ("cells", "grp")
@@ -98,8 +98,9 @@
         self.keep = self.devices * self.pairs * 3 * LANES * 4 <= 1 << 20
         self.fixed_marks = 10
         self.window = min(self.group, 4)
-        self.piece = min(self.cells, 512)
+        self.piece = min(self.cells, 256)
         self.pieces = self.cells // self.piece
+        self.sends = min(self.pieces, 4)
         self.chunk = min(self.cells, PIECE)
         self.chunks = self.cells // self.chunk
 
@@ -635,8 +636,9 @@
     last_copy = pltpu.make_async_copy(centroids, centroids_hbm, done)
     last_copy.start()
     copies = []
-    for c in range(plan.pieces):
-        at = slice(c * plan.piece, (c + 1) * plan.piece)
+    span = plan.cells // plan.sends
+    for c in range(plan.sends):
+        at = slice(c * span, (c + 1) * span)
         copies.append(pltpu.make_async_copy(out.at[:, at], out_hbm.at[:, at], sems.at[c]))
 
     def moved(c, base):
@@ -657,7 +659,8 @@
         for c in range(plan.pieces):
             at = slice(c * plan.piece, (c + 1) * plan.piece)
             out[:, at] = xs[:, at] - moved(c, info[4 + c])
-            copies[c].start()
+            if (c + 1) * plan.sends % plan.pieces == 0:
+                copies[(c + 1) * plan.sends // plan.pieces - 1].start()
 
     @pl.when(sum(more) > 0)
     def general():
@@ -788,7 +791,7 @@
             pltpu.VMEM((k, LANES), f32),
             pltpu.VMEM((plan.dims, cells), f32),
             pltpu.VMEM((k // plan.rows, plan.dims), f32),
-            pltpu.SemaphoreType.DMA((plan.pieces,)),
+            pltpu.SemaphoreType.DMA((plan.sends,)),
             pltpu.SemaphoreType.DMA,
         ],
     )(info, ridges, mine, theirs, a1, a2, moments, places, xs)

time: 32.7 us -> 32.4 us (level)
  Pallas kernels: 5.57 us -> 5.21 us
    pallas_call x1, Pallas kernels: 2.48 us -> 2.08 us  [body(): pl.pallas_call(bound(count_kernel, plan, 'count'), name='count', out_shap...]
where the time goes in v6:
time: 32.4 us; the launch traced here: 32.2 us
  blocking collectives  25 us (77%)
  Pallas kernels  5.21 us (16%)
  waiting for transfers between devices  0.83 us (3%)
  between operations  0.65 us (2%)
  starting transfers between devices  0.51 us (2%)
    all_to_all x1, blocking collectives, body(): ids = hold(lax.all_to_all(send, AXES, 0, 0, tiled=True))  14.3 us
    all_to_all x1, blocking collectives, body(): got = lax.all_to_all(send.reshape(rows, 1, LANES), AXES, 0, 0, tiled=True)  10.7 us
    pallas_call x1, Pallas kernels, body(): pl.pallas_call(bound(count_kernel, plan, 'count'), name='count', out_shap...  2.08 us
    pallas_call x1, Pallas kernels, body(): pl.pallas_call(bound(correct_kernel, plan, 'correct'), name='correct', co...  1.64 us
    pallas_call x1, Pallas kernels, body(): pl.pallas_call(bound(moment_kernel, plan, 'moment'), name='moment', compi...  1.16 us
    ppermute x1, waiting for transfers between devices, body(): theirs = hold(lax.ppermute(theirs, AXES, swap))  0.83 us
  transfers between devices with their start and end apart: 1, of which 1 were waited for; matrix products, arithmetic and copies ran while one was open for 0% of the time, Pallas kernels for 0%

profile of v6, /device:TPU:0, one launch (start us, length us, event | category | flops | bytes accessed | tf_op | source)
XLA Modules:
  0.0 32.2 jit_solution(7712406388171288415)
XLA Ops:
  0.6 2.1 %count.1 = (f32[32,128]{1,0:T(8,128)S(1)}, f32[16,4096]{1,0:T(8,128)S(1)}, f32[7,16,128]{2,1,0:T(8,128)S(1)}, f32[7,128]{1,0:T(8,128)S(1)}, bf16[16,4096]{1,0:T(...) custom-call(s32[200]{0:T(256)} %refs_0_.1, ...), custom_call_target="tpu_custom_call" | custom-call | tf_op jit(solution)/shard_map/count/pallas_call | solution.py:712
  2.7 14.3 %all_to_all.16 = f32[32,1,128]{2,1,0:T(1,128)S(1)} all-to-all(f32[32,1,128]{2,1,0:T(1,128)S(1)} %bitcast.12), channel_id=1, replica_groups=mesh['cells'=8,'grp'=4] {'cells','grp'}, dimensions={0} | all-to-all | bytes 32768 | tf_op jit(solution)/shard_map/all_to_all | solution.py:742
  17.0 1.2 %moment.1 = (f32[384,128]{1,0:T(8,128)S(1)}, bf16[16,4096]{1,0:T(8,128)(2,1)S(1)}, bf16[16,4096]{1,0:T(8,128)(2,1)S(1)}, f32[1920,128]{1,0:T(8,128)S(1)}) custom-call(s32[21]{0:T(128)S(4)} %get-tuple-element.17.refs_0_, f32[112]{0:T(128)S(4)} %get-tuple-element.18.refs_1_, f32[32,128]{1,0:T(8,128)S(1)} %bitcast.10, ...), custom_call_target="tpu_custom_call" | custom-call | tf_op jit(solution)/shard_map/moment/pallas_call | solution.py:743
  18.2 10.7 %all_to_all.17 = f32[384,1,128]{2,1,0:T(1,128)S(1)} all-to-all(f32[384,1,128]{2,1,0:T(1,128)S(1)} %bitcast.9), channel_id=1, replica_groups=mesh['cells'=8,'grp'=4] {'cells','grp'}, dimensions={0} | all-to-all | bytes 393216 | tf_op jit(solution)/shard_map/all_to_all | solution.py:763
  28.8 0.3 %reduce.1 = (f32[4,8,128]{2,1,0:T(8,128)S(1)}, f32[12,128]{1,0:T(8,128)S(1)}) custom-call(s32[21]{0:T(128)S(4)} %get-tuple-element.17.refs_0_, f32[384,128]{1,0:T(8,128)S(1)} %bitcast.8, f32[32,128]{1,0:T(8,128)S(1)} %bitcast.11), custom_call_target="tpu_custom_call" | custom-call | tf_op jit(solution)/shard_map/reduce/pallas_call | solution.py:766
  29.2 0.5 %collective-permute-start = (f32[12,128]{1,0:T(8,128)S(1)}, f32[12,128]{1,0:T(8,128)S(1)}, u32[]{:S(2)}, u32[]{:S(2)}) collective-permute-start(f32[12,128]{1,0:T(8,128)S(1)} %get-tuple-element.27), channel_id=1, source_target_pairs={{0,1},{1,0},{2,3},{3,2},{4,5},{5,4},{6,7},{7,6},{8,9},{9,8},{10,11... | collective-permute-start | bytes 18440 | tf_op jit(solution)/shard_map/ppermute | solution.py:777
  29.7 0.8 %collective-permute-done.refs_3_ = f32[12,128]{1,0:T(8,128)S(1)} collective-permute-done((f32[12,128]{1,0:T(8,128)S(1)}, f32[12,128]{1,0:T(8,128)S(1)}, u32[]{:S(2)}, u32[]{:S(2)}) %collective-permute-start) | collective-permute-done | bytes 6176 | tf_op jit(solution)/shard_map/ppermute | solution.py:777
  30.5 1.6 %correct.1 = (f32[50,4096]{1,0:T(8,128)}, f32[2,50]{1,0:T(2,128)}) custom-call(s32[21]{0:T(128)S(4)} %get-tuple-element.17.refs_0_, f32[112]{0:T(128)S(4)} %get-tuple-element.18.refs_1_, f32[4,8,128]{2,1,0:T(8,128)S(1)} %get-tuple-element.26.refs_2_, f32[12,128]{1,0:T(8,128)S(1)} %collective-permute-done.refs_3_, ...), custom_call_target="tpu_custom_call" | custom-call | tf_op jit(solution)/shard_map/correct/pallas_call | solution.py:778
Async XLA Ops:
  29.2 1.3 %collective-permute-start = (f32[12,128]{1,0:T(8,128)S(1)}, f32[12,128]{1,0:T(8,128)S(1)}, u32[]{:S(2)}, u32[]{:S(2)}) collective-permute-start(f32[12,128]{1,0:T(8,128)S(1)} %get-tuple-element.27), channel_id=1, source_target_pairs={{0,1},{1,0},{2,3},{3,2},{4,5},{5,4},{6,7},{7,6},{8,9},{9,8},{10,11... | collective-permute-start | bytes 18440 | tf_op jit(solution)/shard_map/ppermute | solution.py:777

commit v7 on v6

--- a/solution.py
+++ b/solution.py
@@ -387,48 +387,11 @@
         to = pl.ds(pl.multiple_of(base * k, k), size)
         moments[to, :] = moments[to, :] + (both[0:size] + both[size:])
 
-    more = extra_windows(plan, info)
-
-    @pl.when(tiles == 1)
-    def straight():
-        spare = (TILE + plan.window) * k
-        moments[0:spare, :] = jnp.zeros((spare, LANES), f32)
-        for c in range(plan.chunks):
-            settle(plan.at(c), factor_of(weights, 0, plan.at(c)))
-        for c in range(plan.pieces):
-            collect(c, info[4 + c])
-
-    @pl.when(tiles > 1)
-    def general():
-        def clear(g, carry):
-            moments[pl.ds(pl.multiple_of(g * plan.depth, plan.depth), plan.depth), :] = jnp.zeros(
-                (plan.depth, LANES), f32
-            )
-            return carry
-
-        lax.fori_loop(0, groups + 1, clear, 0)
-        wide[...] = jnp.zeros_like(wide)
-
-        def add(g, carry):
-            weights = factors(g)
-            for c in range(plan.chunks):
-                wide[:, plan.at(c)] += factor_of(weights, g, plan.at(c))
-            return carry
-
-        lax.fori_loop(0, tiles, add, 0)
-        for c in range(plan.chunks):
-            settle(plan.at(c), wide[:, plan.at(c)])
-        for c in range(plan.pieces):
-            collect(c, info[4 + c])
-
-    @pl.when(sum(more) > 0)
-    def others():
-        other_windows(plan, info, more, collect)
-
     sums[...] = jnp.zeros_like(sums)
 
     def gather(g, carry):
-        to = pl.ds(pl.multiple_of(g * plan.depth, plan.depth), plan.depth)
+        start = g * plan.depth if isinstance(g, int) else pl.multiple_of(g * plan.depth, plan.depth)
+        to = pl.ds(start, plan.depth)
         both = moments[to, :]
         both = both + pltpu.roll(both, HALF, 1)
         moments[to, :] = both
@@ -447,7 +410,58 @@
         sums[0], sums[1], sums[2], sums[3] = inner, head, tail, every
         return carry
 
-    lax.fori_loop(0, groups, gather, 0)
+    more = extra_windows(plan, info)
+    simple = (tiles == 1) & (sum(more) == 0)
+
+    def first_windows():
+        spare = (TILE + plan.window) * k
+        moments[0:spare, :] = jnp.zeros((spare, LANES), f32)
+        for c in range(plan.chunks):
+            settle(plan.at(c), factor_of(weights, 0, plan.at(c)))
+        for c in range(plan.pieces):
+            collect(c, info[4 + c])
+
+    @pl.when(simple)
+    def straight():
+        first_windows()
+        for g in range(TILE // plan.group):
+            gather(g, 0)
+
+    @pl.when(jnp.logical_not(simple) & (tiles == 1))
+    def crowded():
+        first_windows()
+
+    @pl.when(tiles > 1)
+    def general():
+        def clear(g, carry):
+            moments[pl.ds(pl.multiple_of(g * plan.depth, plan.depth), plan.depth), :] = jnp.zeros(
+                (plan.depth, LANES), f32
+            )
+            return carry
+
+        lax.fori_loop(0, groups + 1, clear, 0)
+        wide[...] = jnp.zeros_like(wide)
+
+        def add(g, carry):
+            weights = factors(g)
+            for c in range(plan.chunks):
+                wide[:, plan.at(c)] += factor_of(weights, g, plan.at(c))
+            return carry
+
+        lax.fori_loop(0, tiles, add, 0)
+        for c in range(plan.chunks):
+            settle(plan.at(c), wide[:, plan.at(c)])
+        for c in range(plan.pieces):
+            collect(c, info[4 + c])
+
+    @pl.when(sum(more) > 0)
+    def others():
+        other_windows(plan, info, more, collect)
+
+    @pl.when(jnp.logical_not(simple))
+    def looped():
+        lax.fori_loop(0, groups, gather, 0)
+
     inner, head, tail, every = [pack_pairs(sums.at[i]) for i in range(4)]
     lanes = lax.rem(iota(inner.shape, 1), HALF)
     inner = jnp.where(lanes <= plan.dims, inner, 0.0)
@@ -599,7 +613,7 @@
 
     intercept, first_sum, last_sum = both(0), both(1), both(2)
     def slope(g, carry):
-        start = pl.multiple_of(g * plan.depth, plan.depth)
+        start = g * plan.depth if isinstance(g, int) else pl.multiple_of(g * plan.depth, plan.depth)
         held = moments[pl.ds(start, plan.depth), :]
         made = []
         for j in range(plan.group):
@@ -614,10 +628,6 @@
             slopes[i, pl.ds(start, plan.depth), :] = piece
         return carry
 
-    lax.fori_loop(0, groups, slope, 0)
-    blank = jnp.zeros((plan.depth, LANES), bf16)
-    for i in range(2):
-        slopes[i, pl.ds(pl.multiple_of(groups * plan.depth, plan.depth), plan.depth), :] = blank
     size = plan.window * k
 
     rows[...] = mine[3]
@@ -654,16 +664,27 @@
 
     more = extra_windows(plan, info)
 
-    @pl.when(sum(more) == 0)
+    at_once = TILE // plan.group
+    blank = jnp.zeros((plan.depth, LANES), bf16)
+    simple = (sum(more) == 0) & (groups <= at_once)
+
+    @pl.when(simple)
     def straight():
+        for g in range(at_once):
+            slope(g, 0)
+        for i in range(2):
+            slopes[i, at_once * plan.depth : (at_once + 1) * plan.depth, :] = blank
         for c in range(plan.pieces):
             at = slice(c * plan.piece, (c + 1) * plan.piece)
             out[:, at] = xs[:, at] - moved(c, info[4 + c])
             if (c + 1) * plan.sends % plan.pieces == 0:
                 copies[(c + 1) * plan.sends // plan.pieces - 1].start()
 
-    @pl.when(sum(more) > 0)
+    @pl.when(jnp.logical_not(simple))
     def general():
+        lax.fori_loop(0, groups, slope, 0)
+        for i in range(2):
+            slopes[i, pl.ds(pl.multiple_of(groups * plan.depth, plan.depth), plan.depth), :] = blank
         for c in range(plan.pieces):
             at = slice(c * plan.piece, (c + 1) * plan.piece)
             out[:, at] = xs[:, at] - moved(c, info[4 + c])

time: 32.4 us -> 32.4 us (level)
  no operation moved by 1% of the time
where the time goes in v7:
time: 32.4 us; the launch traced here: 32.2 us
  blocking collectives  25.1 us (77%)
  Pallas kernels  5.17 us (16%)
  waiting for transfers between devices  0.83 us (3%)
  between operations  0.65 us (2%)
  starting transfers between devices  0.51 us (2%)
    all_to_all x1, blocking collectives, body(): ids = hold(lax.all_to_all(send, AXES, 0, 0, tiled=True))  14.4 us
    all_to_all x1, blocking collectives, body(): got = lax.all_to_all(send.reshape(rows, 1, LANES), AXES, 0, 0, tiled=True)  10.7 us
    pallas_call x1, Pallas kernels, body(): pl.pallas_call(bound(count_kernel, plan, 'count'), name='count', out_shap...  2.07 us
    pallas_call x1, Pallas kernels, body(): pl.pallas_call(bound(correct_kernel, plan, 'correct'), name='correct', co...  1.59 us
    pallas_call x1, Pallas kernels, body(): pl.pallas_call(bound(moment_kernel, plan, 'moment'), name='moment', compi...  1.17 us
    ppermute x1, waiting for transfers between devices, body(): theirs = hold(lax.ppermute(theirs, AXES, swap))  0.83 us
  transfers between devices with their start and end apart: 1, of which 1 were waited for; matrix products, arithmetic and copies ran while one was open for 0% of the time, Pallas kernels for 0%

profile of v7, /device:TPU:0, one launch (start us, length us, event | category | flops | bytes accessed | tf_op | source)
XLA Modules:
  0.0 32.2 jit_solution(8625707046633697572)
XLA Ops:
  0.6 2.1 %count.1 = (f32[32,128]{1,0:T(8,128)S(1)}, f32[16,4096]{1,0:T(8,128)S(1)}, f32[7,16,128]{2,1,0:T(8,128)S(1)}, f32[7,128]{1,0:T(8,128)S(1)}, bf16[16,4096]{1,0:T(...) custom-call(s32[200]{0:T(256)} %refs_0_.1, ...), custom_call_target="tpu_custom_call" | custom-call | tf_op jit(solution)/shard_map/count/pallas_call | solution.py:733
  2.7 14.4 %all_to_all.16 = f32[32,1,128]{2,1,0:T(1,128)S(1)} all-to-all(f32[32,1,128]{2,1,0:T(1,128)S(1)} %bitcast.12), channel_id=1, replica_groups=mesh['cells'=8,'grp'=4] {'cells','grp'}, dimensions={0} | all-to-all | bytes 32768 | tf_op jit(solution)/shard_map/all_to_all | solution.py:763
  17.1 1.2 %moment.1 = (f32[384,128]{1,0:T(8,128)S(1)}, bf16[16,4096]{1,0:T(8,128)(2,1)S(1)}, bf16[16,4096]{1,0:T(8,128)(2,1)S(1)}, f32[1920,128]{1,0:T(8,128)S(1)}) custom-call(s32[21]{0:T(128)S(4)} %get-tuple-element.17.refs_0_, f32[112]{0:T(128)S(4)} %get-tuple-element.18.refs_1_, f32[32,128]{1,0:T(8,128)S(1)} %bitcast.10, ...), custom_call_target="tpu_custom_call" | custom-call | tf_op jit(solution)/shard_map/moment/pallas_call | solution.py:764
  18.3 10.7 %all_to_all.17 = f32[384,1,128]{2,1,0:T(1,128)S(1)} all-to-all(f32[384,1,128]{2,1,0:T(1,128)S(1)} %bitcast.9), channel_id=1, replica_groups=mesh['cells'=8,'grp'=4] {'cells','grp'}, dimensions={0} | all-to-all | bytes 393216 | tf_op jit(solution)/shard_map/all_to_all | solution.py:784
  29.0 0.3 %reduce.1 = (f32[4,8,128]{2,1,0:T(8,128)S(1)}, f32[12,128]{1,0:T(8,128)S(1)}) custom-call(s32[21]{0:T(128)S(4)} %get-tuple-element.17.refs_0_, f32[384,128]{1,0:T(8,128)S(1)} %bitcast.8, f32[32,128]{1,0:T(8,128)S(1)} %bitcast.11), custom_call_target="tpu_custom_call" | custom-call | tf_op jit(solution)/shard_map/reduce/pallas_call | solution.py:787
  29.3 0.5 %collective-permute-start = (f32[12,128]{1,0:T(8,128)S(1)}, f32[12,128]{1,0:T(8,128)S(1)}, u32[]{:S(2)}, u32[]{:S(2)}) collective-permute-start(f32[12,128]{1,0:T(8,128)S(1)} %get-tuple-element.27), channel_id=1, source_target_pairs={{0,1},{1,0},{2,3},{3,2},{4,5},{5,4},{6,7},{7,6},{8,9},{9,8},{10,11... | collective-permute-start | bytes 18440 | tf_op jit(solution)/shard_map/ppermute | solution.py:798
  29.8 0.8 %collective-permute-done.refs_3_ = f32[12,128]{1,0:T(8,128)S(1)} collective-permute-done((f32[12,128]{1,0:T(8,128)S(1)}, f32[12,128]{1,0:T(8,128)S(1)}, u32[]{:S(2)}, u32[]{:S(2)}) %collective-permute-start) | collective-permute-done | bytes 6176 | tf_op jit(solution)/shard_map/ppermute | solution.py:798
  30.7 1.6 %correct.1 = (f32[50,4096]{1,0:T(8,128)}, f32[2,50]{1,0:T(2,128)}) custom-call(s32[21]{0:T(128)S(4)} %get-tuple-element.17.refs_0_, f32[112]{0:T(128)S(4)} %get-tuple-element.18.refs_1_, f32[4,8,128]{2,1,0:T(8,128)S(1)} %get-tuple-element.26.refs_2_, f32[12,128]{1,0:T(8,128)S(1)} %collective-permute-done.refs_3_, ...), custom_call_target="tpu_custom_call" | custom-call | tf_op jit(solution)/shard_map/correct/pallas_call | solution.py:799
Async XLA Ops:
  29.3 1.3 %collective-permute-start = (f32[12,128]{1,0:T(8,128)S(1)}, f32[12,128]{1,0:T(8,128)S(1)}, u32[]{:S(2)}, u32[]{:S(2)}) collective-permute-start(f32[12,128]{1,0:T(8,128)S(1)} %get-tuple-element.27), channel_id=1, source_target_pairs={{0,1},{1,0},{2,3},{3,2},{4,5},{5,4},{6,7},{7,6},{8,9},{9,8},{10,11... | collective-permute-start | bytes 18440 | tf_op jit(solution)/shard_map/ppermute | solution.py:798

commit v8 on v7

--- a/solution.py
+++ b/solution.py
@@ -243,8 +243,8 @@
         x1, x2, x3 = split(x, 3)
         parts[0:HALF, at] = x1
         parts[HALF:, at] = x2
-        stacked = jnp.concatenate([x1, x2, x3, jnp.zeros_like(x1)], axis=0)
-        dots = jnp.dot(weights, stacked, preferred_element_type=f32)
+        stacked = jnp.concatenate([x1, x2, x3], axis=0)
+        dots = jnp.dot(weights[:, 0 : 3 * HALF], stacked, preferred_element_type=f32)
         dots = dots[0:k] + dots[k : 2 * k] + dots[2 * k : 3 * k]
         return (2.0 * dots - lengths) * inverse
 
@@ -363,13 +363,13 @@
         ratio = jnp.where(lane < TILE, ratio * ratio, 0.0)
         w1, w2, w3 = [part.astype(f32) for part in split(ratio, 3)]
         row = w1 + pltpu.roll(w2, TILE, 1) + pltpu.roll(w3, 2 * TILE, 1)
-        return row.astype(bf16)[:, 0 : 4 * TILE]
+        return row.astype(bf16)[:, 0 : 3 * TILE]
 
     def factor_of(weights, g, at):
         shape = (TILE, at.stop - at.start)
         rows = (iota(shape, 0) + g * TILE).astype(f32).astype(bf16)
         hot = jnp.where(places[:, at] == rows, bf16(1), bf16(0))
-        hot = jnp.concatenate([hot, hot, hot, jnp.zeros_like(hot)], axis=0)
+        hot = jnp.concatenate([hot, hot, hot], axis=0)
         return jnp.dot(weights, hot, preferred_element_type=f32)
 
     weights = factors(0)

time: 32.4 us -> 32.3 us (level)
  no operation moved by 1% of the time
where the time goes in v8:
time: 32.3 us; the launch traced here: 32.1 us
  blocking collectives  24.9 us (77%)
  Pallas kernels  5.28 us (16%)
  waiting for transfers between devices  0.83 us (3%)
  between operations  0.65 us (2%)
  starting transfers between devices  0.51 us (2%)
    all_to_all x1, blocking collectives, body(): ids = hold(lax.all_to_all(send, AXES, 0, 0, tiled=True))  14.2 us
    all_to_all x1, blocking collectives, body(): got = lax.all_to_all(send.reshape(rows, 1, LANES), AXES, 0, 0, tiled=True)  10.7 us
    pallas_call x1, Pallas kernels, body(): pl.pallas_call(bound(count_kernel, plan, 'count'), name='count', out_shap...  2.18 us
    pallas_call x1, Pallas kernels, body(): pl.pallas_call(bound(correct_kernel, plan, 'correct'), name='correct', co...  1.59 us
    pallas_call x1, Pallas kernels, body(): pl.pallas_call(bound(moment_kernel, plan, 'moment'), name='moment', compi...  1.17 us
    ppermute x1, waiting for transfers between devices, body(): theirs = hold(lax.ppermute(theirs, AXES, swap))  0.83 us
  transfers between devices with their start and end apart: 1, of which 1 were waited for; matrix products, arithmetic and copies ran while one was open for 0% of the time, Pallas kernels for 0%

profile of v8, /device:TPU:0, one launch (start us, length us, event | category | flops | bytes accessed | tf_op | source)
XLA Modules:
  0.0 32.1 jit_solution(10030230048517952499)
XLA Ops:
  0.6 2.2 %count.1 = (f32[32,128]{1,0:T(8,128)S(1)}, f32[16,4096]{1,0:T(8,128)S(1)}, f32[7,16,128]{2,1,0:T(8,128)S(1)}, f32[7,128]{1,0:T(8,128)S(1)}, bf16[16,4096]{1,0:T(...) custom-call(s32[200]{0:T(256)} %refs_0_.1, ...), custom_call_target="tpu_custom_call" | custom-call | tf_op jit(solution)/shard_map/count/pallas_call | solution.py:733
  2.8 14.2 %all_to_all.16 = f32[32,1,128]{2,1,0:T(1,128)S(1)} all-to-all(f32[32,1,128]{2,1,0:T(1,128)S(1)} %bitcast.12), channel_id=1, replica_groups=mesh['cells'=8,'grp'=4] {'cells','grp'}, dimensions={0} | all-to-all | bytes 32768 | tf_op jit(solution)/shard_map/all_to_all | solution.py:763
  17.0 1.2 %moment.1 = (f32[384,128]{1,0:T(8,128)S(1)}, bf16[16,4096]{1,0:T(8,128)(2,1)S(1)}, bf16[16,4096]{1,0:T(8,128)(2,1)S(1)}, f32[1920,128]{1,0:T(8,128)S(1)}) custom-call(s32[21]{0:T(128)S(4)} %get-tuple-element.17.refs_0_, f32[112]{0:T(128)S(4)} %get-tuple-element.18.refs_1_, f32[32,128]{1,0:T(8,128)S(1)} %bitcast.10, ...), custom_call_target="tpu_custom_call" | custom-call | tf_op jit(solution)/shard_map/moment/pallas_call | solution.py:764
  18.2 10.7 %all_to_all.17 = f32[384,1,128]{2,1,0:T(1,128)S(1)} all-to-all(f32[384,1,128]{2,1,0:T(1,128)S(1)} %bitcast.9), channel_id=1, replica_groups=mesh['cells'=8,'grp'=4] {'cells','grp'}, dimensions={0} | all-to-all | bytes 393216 | tf_op jit(solution)/shard_map/all_to_all | solution.py:784
  28.9 0.3 %reduce.1 = (f32[4,8,128]{2,1,0:T(8,128)S(1)}, f32[12,128]{1,0:T(8,128)S(1)}) custom-call(s32[21]{0:T(128)S(4)} %get-tuple-element.17.refs_0_, f32[384,128]{1,0:T(8,128)S(1)} %bitcast.8, f32[32,128]{1,0:T(8,128)S(1)} %bitcast.11), custom_call_target="tpu_custom_call" | custom-call | tf_op jit(solution)/shard_map/reduce/pallas_call | solution.py:787
  29.2 0.5 %collective-permute-start = (f32[12,128]{1,0:T(8,128)S(1)}, f32[12,128]{1,0:T(8,128)S(1)}, u32[]{:S(2)}, u32[]{:S(2)}) collective-permute-start(f32[12,128]{1,0:T(8,128)S(1)} %get-tuple-element.27), channel_id=1, source_target_pairs={{0,1},{1,0},{2,3},{3,2},{4,5},{5,4},{6,7},{7,6},{8,9},{9,8},{10,11... | collective-permute-start | bytes 18440 | tf_op jit(solution)/shard_map/ppermute | solution.py:798
  29.7 0.8 %collective-permute-done.refs_3_ = f32[12,128]{1,0:T(8,128)S(1)} collective-permute-done((f32[12,128]{1,0:T(8,128)S(1)}, f32[12,128]{1,0:T(8,128)S(1)}, u32[]{:S(2)}, u32[]{:S(2)}) %collective-permute-start) | collective-permute-done | bytes 6176 | tf_op jit(solution)/shard_map/ppermute | solution.py:798
  30.5 1.6 %correct.1 = (f32[50,4096]{1,0:T(8,128)}, f32[2,50]{1,0:T(2,128)}) custom-call(s32[21]{0:T(128)S(4)} %get-tuple-element.17.refs_0_, f32[112]{0:T(128)S(4)} %get-tuple-element.18.refs_1_, f32[4,8,128]{2,1,0:T(8,128)S(1)} %get-tuple-element.26.refs_2_, f32[12,128]{1,0:T(8,128)S(1)} %collective-permute-done.refs_3_, ...), custom_call_target="tpu_custom_call" | custom-call | tf_op jit(solution)/shard_map/correct/pallas_call | solution.py:799
Async XLA Ops:
  29.2 1.3 %collective-permute-start = (f32[12,128]{1,0:T(8,128)S(1)}, f32[12,128]{1,0:T(8,128)S(1)}, u32[]{:S(2)}, u32[]{:S(2)}) collective-permute-start(f32[12,128]{1,0:T(8,128)S(1)} %get-tuple-element.27), channel_id=1, source_target_pairs={{0,1},{1,0},{2,3},{3,2},{4,5},{5,4},{6,7},{7,6},{8,9},{9,8},{10,11... | collective-permute-start | bytes 18440 | tf_op jit(solution)/shard_map/ppermute | solution.py:798
